TPU v7x, 32 devices: a whole 2x2x4 slice. The times are simulated.
32 devices in a mesh: grp: 2 (over x), gx: 4 (over z), gy: 4 (over y, core).
Axes of the slice: x: 2, y: 2, z: 4, core: 2. Of those that a mesh axis runs over, the one named last changes fastest.
Arguments:
- state: float32 [2, 3, 144, 192, 90], P('grp', None, 'gx', 'gy'), may hold values from -6 to 6
- courant: float32 [2, 144, 192, 90], P('grp', 'gx', 'gy'), may hold values from 0.15 to 0.5
- vert_inverse: float32 [2, 90, 90], P('grp'), may hold values from -0.1 to 0.65, as said below
- interp_index: int32 [144, 192, 4], P('gx', 'gy'), may hold values from 0 to 8
- interp_weight: float32 [144, 192, 4], P('gx', 'gy'), may hold values from 0.2 to 1
- restrict_index: int32 [48, 64, 9], P('gx', 'gy'), may hold values from 0 to 8
- restrict_weight: float32 [48, 64, 9], P('gx', 'gy'), may hold values from 0.2 to 1
Outputs:
- new_state: float32 [2, 3, 144, 192, 90], P('grp', None, 'gx', 'gy')
Inputs may be any that keep to these rules, and one draw needn't show every extreme that they name: `vert_inverse`: each matrix's diagonal lies in 0.5 to 0.65, its neighbours on the diagonal beside it in 0.05 to 0.12, the rest is small.
All inputs are finite; a program needn't handle non-finite values.
Results may differ from a plain program's by a relative error of at most 0.0001.
Values sent between devices are 32-bit elements; how exact they have to be, the bound alone decides.
A program may use at most 128 MiB of HBM per device.

v0:
```python
import functools

import jax
import jax.numpy as jnp
from jax import lax
from jax.experimental import pallas as pl
from jax.experimental.pallas import tpu as pltpu
from jax.sharding import PartitionSpec as P

SUBS = 4
BAND = 5
FEEDBACK = 0.5
MESH = pl.DeviceIdType.MESH
F32 = jnp.float32
XB, YB = 2, 8


def split(a):
    high = a.astype(jnp.bfloat16)
    return high, (a - high.astype(F32)).astype(jnp.bfloat16)


def dot(a, b):
    return jnp.dot(a, b, preferred_element_type=F32)


def dot3(a, b_high, b_low):
    a_high, a_low = split(a)
    return dot(a_high, b_high) + (dot(a_low, b_high) + dot(a_high, b_low))


def third(t):
    return (t * 11) >> 5


def dense(cells, shares, depth):
    places = lax.broadcasted_iota(jnp.int32, (depth, cells[0].shape[1]), 0)
    total = jnp.zeros(places.shape, F32)
    for cell, share in zip(cells, shares):
        total = total + jnp.where(places == cell, share, 0.0)
    return total.T


def kernel(
    cx, cy,
    state, courant, *rest,
):
    small, (
    S,
    C, inverse, iidx, iwgt, ridx, rwgt, mean, wr, wx, wy, sx0, sy0, rx0, ry0, sx, sy, rx, ry, rst, fb, xstrip, ystrip,
    load_sem, halo_send, halo_recv, strip_send, strip_recv, fb_send, fb_recv,
    q0, q1, q2, q3, q_send, q_recv,
    ) = rest[:5], rest[5:]
    g, a, b = lax.axis_index("grp"), lax.axis_index("gx"), lax.axis_index("gy")
    nx, ny, lev = state.shape[2], state.shape[3], state.shape[4]
    tx, ty = nx // 3, ny // 3
    fx, fy = cx // 2, cy // 2

    barrier = pltpu.get_barrier_semaphore()
    greeted = []

    def greet(on, device):
        greeted.append(on)

        @pl.when(on)
        def _():
            pl.semaphore_signal(barrier, inc=1, device_id=device, device_id_type=MESH)

    greet(a > 0, (g, a - 1, b))
    greet(a < cx - 1, (g, a + 1, b))
    greet(b > 0, (g, a, b - 1))
    greet(b < cy - 1, (g, a, b + 1))
    for i in range(-1, 4):
        for j in range(-1, 4):
            child_a, child_b = 3 * (a - fx) + i, 3 * (b - fy) + j
            greet(
                (g == 0) & (a >= fx) & (b >= fy) & (child_a >= 0) & (child_a < cx)
                & (child_b >= 0) & (child_b < cy),
                (1, child_a, child_b),
            )

    def parents(place, first, count):
        own = first + place // 3
        return (
            (place >= 0, own),
            ((place % 3 == 0) & (place > 0), own - 1),
            ((place % 3 == 2) & (own + 1 < count), own + 1),
        )

    for on_a, parent_a in parents(a, fx, cx):
        for on_b, parent_b in parents(b, fy, cy):
            greet((g == 1) & on_a & on_b, (0, parent_a, parent_b))

    def route(at_a, at_b):
        to_a, to_b = fx + at_a // 3, fy + at_b // 3
        far = (at_a != to_a) & (at_b != to_b)
        direct = (at_a == to_a) & (at_b == to_b)
        by_nest = (at_a % 3 == 1) & (at_b == to_b) & (at_a != to_a)
        over = jnp.logical_not(direct | by_nest)
        along_a = over & (at_a % 3 == 1) & far
        along_b = over & (at_a % 3 == 0) & far
        last = over & jnp.logical_not(along_a | along_b)
        return to_a, to_b, direct, by_nest, over, along_a, along_b, last

    to_a, to_b, direct, by_nest, over, along_a, along_b, last = route(a, b)
    parent, nest = g == 0, g == 1
    mid_a = 3 * (a - fx) + 1
    comes = (a >= fx) & (mid_a < cx)
    middle = route(mid_a, b)
    relay1, relay3 = parent & comes & middle[5], nest & comes & middle[3]
    relay2 = []
    for j in range(3):
        side_b = 3 * (b - fy) + j
        relay2.append((parent & (b >= fy) & (side_b < cy) & route(a, side_b)[6], side_b))
    greet(nest & over, (0, a, b))
    greet(parent & over, (1, a, b))
    greet(parent & along_a, (0, to_a, b))
    greet(relay1, (0, mid_a, b))
    greet(parent & along_b, (0, a, to_b))
    for on, side_b in relay2:
        greet(on, (0, a, side_b))
        greet(on, (0, to_a, b))
    greet(nest & by_nest, (1, to_a, b))
    greet(relay3, (1, mid_a, b))
    greet(parent & last, (0, to_a, to_b))
    greet(relay1, (0, a, to_b))
    greet(relay3, (0, a, b))
    greet(nest & direct, (0, a, b))
    for i in range(3):
        for j in range(3):
            from_a, from_b = 3 * (a - fx) + i, 3 * (b - fy) + j
            on = parent & (a >= fx) & (b >= fy) & (from_a < cx) & (from_b < cy)
            _, _, f_direct, f_nest, _, f_a, f_b, f_last = route(from_a, from_b)
            greet(on & f_direct, (1, a, b))
            greet(on & f_nest, (1, a, from_b))
            greet(on & f_a, (0, a, from_b))
            greet(on & f_b, (0, from_a, b))
            greet(on & f_last, (0, from_a, from_b))

    loads = [
        pltpu.make_async_copy(
            state.at[0], S.at[:, pl.ds(XB, nx), pl.ds(YB, ny), :], load_sem.at[0]
        ),
        pltpu.make_async_copy(
            courant.at[0], C.at[pl.ds(1, nx), pl.ds(YB, ny), :], load_sem.at[1]
        ),
    ]
    for n, (src, dst) in enumerate(zip(small, (inverse, iidx, iwgt, ridx, rwgt))):
        loads.append(pltpu.make_async_copy(src, dst, load_sem.at[2 + n]))
    for copy in loads:
        copy.start()
    zrow = jnp.zeros((2, ny, lev), F32)
    S[0, 0:2, YB : YB + ny, :] = zrow
    S[0, XB + nx : XB + nx + 2, YB : YB + ny, :] = zrow
    S[1, 0:2, YB : YB + ny, :] = zrow
    S[1, XB + nx : XB + nx + 2, YB : YB + ny, :] = zrow
    C[0:1, YB : YB + ny, :] = zrow[0:1]
    C[nx + 1 : nx + 2, YB : YB + ny, :] = zrow[0:1]
    zcol = jnp.zeros((nx, 8, lev), F32)
    for c in (0, 2):
        S[c, XB : XB + nx, 0:YB, :] = zcol
        S[c, XB : XB + nx, YB + ny : YB + ny + 8, :] = zcol
    C[1 : 1 + nx, 0:YB, :] = zcol
    C[1 : 1 + nx, YB + ny : YB + ny + 8, :] = zcol
    for copy in loads:
        copy.wait()
    m_high, m_low = split(inverse[:, 0, :])
    pl.semaphore_wait(barrier, sum(on.astype(jnp.int32) for on in greeted))

    dirs = (
        (a > 0, a < cx - 1, (g, a - 1, b)),
        (a < cx - 1, a > 0, (g, a + 1, b)),
        (b > 0, b < cy - 1, (g, a, b - 1)),
        (b < cy - 1, b > 0, (g, a, b + 1)),
    )

    def halo_copy(k, d):
        if k == 0:
            src, dst = (sx0, rx0) if d < 2 else (sy0, ry0)
            src, dst = src.at[d % 2], dst.at[d % 2]
        else:
            src, dst = (sx, rx) if d < 2 else (sy, ry)
            src, dst = src.at[k - 1, d % 2], dst.at[k - 1, d % 2]
        return pltpu.make_async_remote_copy(
            src_ref=src, dst_ref=dst,
            send_sem=halo_send.at[k, d], recv_sem=halo_recv.at[k, d],
            device_id=dirs[d][2], device_id_type=MESH,
        )

    def exchange(k):
        cols = slice(YB, YB + ny)
        rows = slice(XB, XB + nx)
        last_x, last_y = XB + nx, YB + ny
        if k == 0:
            sx0[0, 0:2] = S[0, XB : XB + 2, cols, :]
            sx0[0, 2:3] = S[1, XB : XB + 1, cols, :]
            sx0[0, 3:4] = C[1:2, cols, :]
            sx0[1, 0:2] = S[0, last_x - 2 : last_x, cols, :]
            sx0[1, 2:3] = S[1, last_x - 1 : last_x, cols, :]
            sx0[1, 3:4] = C[nx : nx + 1, cols, :]
            sy0[0, :, 0:2] = S[0, rows, YB : YB + 2, :]
            sy0[0, :, 2:3] = S[2, rows, YB : YB + 1, :]
            sy0[0, :, 3:4] = C[1 : 1 + nx, YB : YB + 1, :]
            sy0[1, :, 0:2] = S[0, rows, last_y - 2 : last_y, :]
            sy0[1, :, 2:3] = S[2, rows, last_y - 1 : last_y, :]
            sy0[1, :, 3:4] = C[1 : 1 + nx, last_y - 1 : last_y, :]
        else:
            sx[k - 1, 0] = S[0, XB : XB + 2, cols, :]
            sx[k - 1, 1] = S[0, last_x - 2 : last_x, cols, :]
            sy[k - 1, 0] = S[0, rows, YB : YB + 2, :]
            sy[k - 1, 1] = S[0, rows, last_y - 2 : last_y, :]
        for d in range(4):
            @pl.when(dirs[d][0])
            def _():
                halo_copy(k, d).start()
        if k == 0:
            @pl.when(g == 1)
            def _():
                weights()
        for d in range(4):
            @pl.when(dirs[d][1])
            def _():
                halo_copy(k, d).wait_recv()
                if d < 2:
                    got = rx0.at[d] if k == 0 else rx.at[k - 1, d]
                    at = last_x if d == 0 else XB - 2
                    S[0, at : at + 2, cols, :] = got[0:2]
                    if k == 0:
                        at = last_x if d == 0 else XB - 1
                        S[1, at : at + 1, cols, :] = got[2:3]
                        C[at - 1 : at, cols, :] = got[3:4]
                else:
                    got = ry0.at[d - 2] if k == 0 else ry.at[k - 1, d - 2]
                    at = last_y if d == 2 else YB - 2
                    S[0, rows, at : at + 2, :] = got[:, 0:2]
                    if k == 0:
                        at = last_y if d == 2 else YB - 1
                        S[2, rows, at : at + 1, :] = got[:, 2:3]
                        C[1 : 1 + nx, at : at + 1, :] = got[:, 3:4]

    def add_mean(k, c, x, value):
        mean[c, x] = value if k == 0 else mean[c, x] + value

    def winds(k):
        def u_row(r, _):
            slope = 0.5 * (S[0, r + 1, YB : YB + ny, :] - S[0, r - 1, YB : YB + ny, :])
            S[1, r, YB : YB + ny, :] = S[1, r, YB : YB + ny, :] - C[r - 1, YB : YB + ny, :] * slope
            return 0

        u_row(XB - 1, 0)
        u_row(XB + nx, 0)

        cols, wide = slice(YB, YB + ny), slice(YB - 1, YB + ny + 1)
        group = 4

        def rows(i, _):
            new = []
            for j in range(group):
                x = i * group + j
                r = x + XB
                slope = 0.5 * (S[0, r + 1, cols, :] - S[0, r - 1, cols, :])
                u = S[1, r, cols, :] - C[x + 1, cols, :] * slope
                slope = 0.5 * (S[0, r, YB : YB + ny + 2, :] - S[0, r, YB - 2 : YB + ny, :])
                v = S[2, r, wide, :] - C[x + 1, wide, :] * slope
                new.append((x, u, v))
            for x, u, v in new:
                S[1, x + XB, cols, :] = u
                S[2, x + XB, wide, :] = v
                add_mean(k, 1, x, u)
                add_mean(k, 2, x, v[1 : ny + 1])
            return 0

        lax.fori_loop(0, nx // group, rows, 0)

    def press(k):
        group = 12

        def rows(i, _):
            parts = []
            for j in range(group):
                x = i * group + j
                r = x + XB
                div = 0.5 * (S[1, r + 1, YB : YB + ny, :] - S[1, r - 1, YB : YB + ny, :]) + 0.5 * (
                    S[2, r, YB + 1 : YB + ny + 1, :] - S[2, r, YB - 1 : YB + ny - 1, :]
                )
                parts.append(S[0, r, YB : YB + ny, :] - C[x + 1, YB : YB + ny, :] * div)
            solved = dot3(jnp.concatenate(parts, axis=0), m_high, m_low)
            for j in range(group):
                x = i * group + j
                new = solved[j * ny : (j + 1) * ny]
                S[0, x + XB, YB : YB + ny, :] = new
                add_mean(k, 0, x, new)
            return 0

        lax.fori_loop(0, nx // group, rows, 0)

    def hop(src, dst, device, send, recv):
        return pltpu.make_async_remote_copy(
            src_ref=src, dst_ref=dst, send_sem=send, recv_sem=recv,
            device_id=device, device_id_type=MESH,
        )

    def home(src, c, i, j, device, send):
        n = 3 * i + j
        return hop(src, fb.at[n, c], device, send, fb_recv.at[n, c])

    def fb_copies(c):
        mine, sem = rst.at[c], fb_send.at[c]
        return (
            (direct, home(mine, c, a % 3, b % 3, (0, a, b), sem)),
            (by_nest, hop(mine, q3.at[c], (1, to_a, b), sem, q_recv.at[5, c])),
            (over, hop(mine, q0.at[c], (0, a, b), sem, q_recv.at[0, c])),
        )

    def fb_start(c):
        for on, copy in fb_copies(c):
            @pl.when(on)
            def _():
                copy.start()

    def relays(c):
        sem0 = q_send.at[0, c]
        yield parent & over, q0.at[c], 0, (
            (along_a, hop(q0.at[c], q1.at[c], (0, to_a, b), sem0, q_recv.at[1, c])),
            (along_b, hop(q0.at[c], q2.at[b % 3, c], (0, a, to_b), sem0,
                          q_recv.at[2 + b % 3, c])),
            (last, home(q0.at[c], c, a % 3, b % 3, (0, to_a, to_b), sem0)),
        )
        yield relay1, q1.at[c], 1, (
            (relay1, home(q1.at[c], c, 1, b % 3, (0, a, to_b), q_send.at[1, c])),
        )
        for j, (on, side_b) in enumerate(relay2):
            yield on, q2.at[j, c], 2 + j, (
                (on, home(q2.at[j, c], c, 0, j, (0, to_a, b), q_send.at[2 + j, c])),
            )
        yield relay3, q3.at[c], 5, (
            (relay3, home(q3.at[c], c, 1, b % 3, (0, a, b), q_send.at[5, c])),
        )

    def pass_on():
        for c in (1, 2, 0):
            for here, buffer, n, onward in relays(c):
                @pl.when(here)
                def _():
                    hop(buffer, buffer, (g, a, b), q_send.at[n, c], q_recv.at[n, c]).wait_recv()
                    for on, copy in onward:
                        @pl.when(on)
                        def _():
                            copy.start()

    def passed_on():
        for c in (1, 2, 0):
            for here, buffer, n, onward in relays(c):
                @pl.when(here)
                def _():
                    hop(buffer, buffer, (g, a, b), q_send.at[n, c], q_recv.at[n, c]).wait_send()

    def restrict(comps):
        group = 4

        def rows(i, _):
            new = []
            for j in range(group):
                u = i * group + j
                w_high, w_low = split(wr[u])
                for c in comps:
                    block = mean[c, pl.ds(3 * u, 3)].reshape(3 * ny, lev)
                    b_high, b_low = split(block)
                    both = dot(w_high, b_high) + (dot(w_low, b_high) + dot(w_high, b_low))
                    new.append((c, u, both))
            for c, u, both in new:
                rst[c, u] = both
            return 0

        lax.fori_loop(0, tx // group, rows, 0)

    def row_sum(rows):
        total = rows[0]
        for row in rows[1:]:
            total = total + row
        return total

    def weights():
        x_low, x_high = a == 0, a == cx - 1
        y_low, y_high = b == 0, b == cy - 1

        def restrict_row(u, _):
            terms = range(ridx.shape[0])
            w = [rwgt[k, pl.ds(u, 1), :] for k in terms]
            scale = (1.0 / SUBS) / row_sum(w)
            over = [third(ridx[k, pl.ds(u, 1), :]) for k in terms]
            v3 = 3 * lax.broadcasted_iota(jnp.int32, (1, ty), 1)
            cells = [
                over[k] * (ny - 3) + ridx[k, pl.ds(u, 1), :] + v3 for k in terms
            ]
            wr[u] = dense(cells, [part * scale for part in w], 3 * ny)
            return 0

        lax.fori_loop(0, tx, restrict_row, 0)

        def boundary_row(x, cols, origin_x, origin_y, width, depth):
            w = [iwgt[x, k : k + 1, cols] for k in range(4)]
            scale = 1.0 / row_sum(w)
            y = cols.start + lax.broadcasted_iota(jnp.int32, w[0].shape, 1)
            y3 = (y * 171) >> 9
            cells = []
            for k in range(4):
                t = iidx[x, k : k + 1, cols]
                over = third(t)
                source_x = jnp.clip(a * tx + x // 3 + over - 1, 0, cx * tx - 1) - origin_x
                source_y = jnp.clip(b * ty + y3 + (t - 3 * over) - 1, 0, cy * ty - 1) - origin_y
                cells.append(source_x * width + source_y)
            return dense(cells, [part * scale for part in w], depth)

        def y_weights(col, strip0):
            def row(x, _):
                wy[x] = boundary_row(
                    x, slice(col, col + 8), a * tx + x // 3 - 1, b * ty + strip0, 8, 24
                )
                return 0

            lax.fori_loop(0, nx, row, 0)

        def x_weights(first, strip0):
            def row(i, _):
                wx[i] = boundary_row(
                    first + i, slice(0, ny), a * tx + strip0, b * ty - 8, ty + 16, 3 * (ty + 16)
                )
                return 0

            lax.fori_loop(0, BAND, row, 0)

        @pl.when(y_low)
        def _():
            y_weights(0, 0)

        @pl.when(y_high)
        def _():
            y_weights(ny - 8, ty - 8)

        @pl.when(x_low)
        def _():
            x_weights(0, 0)

        @pl.when(x_high)
        def _():
            x_weights(nx - BAND, tx - 3)

    for k in range(SUBS):
        exchange(k)
        winds(k)
        if k == SUBS - 1:
            @pl.when(g == 1)
            def _():
                restrict((1, 2))
                fb_start(1)
                fb_start(2)
        press(k)

    x_windows = {-1: (0, 8, 24), 0: (0, ty + 8, 8), 1: (ty - 8, 2 * ty + 8, 0),
                 2: (2 * ty - 8, ny, 0), 3: (ny - 8, ny, 0)}
    y_windows = {-1: (0, 1, tx + 1), 0: (0, tx + 1, 1), 1: (tx - 1, 2 * tx + 1, 0),
                 2: (2 * tx - 1, nx, 0), 3: (nx - 1, nx, 0)}
    kinds = {-1: 1, 0: 0, 1: 0, 2: 0, 3: 2}

    def strip_copies():
        for side in range(2):
            edge = 0 if side == 0 else cx - 1
            at = XB if side == 0 else XB + tx * (edge % 3) + tx - 3
            for j in range(-1, 4):
                lo, hi, dst = x_windows[j]
                child = 3 * (b - fy) + j
                on = (a == fx + edge // 3) & (b >= fy) & (child >= 0) & (child < cy)
                yield on, pltpu.make_async_remote_copy(
                    src_ref=S.at[:, pl.ds(at, 3), pl.ds(YB + lo, hi - lo), :],
                    dst_ref=xstrip.at[:, :, pl.ds(dst, hi - lo), :],
                    send_sem=strip_send.at[0, side, j + 1], recv_sem=strip_recv.at[0, kinds[j]],
                    device_id=(1, edge, child), device_id_type=MESH,
                )
            edge = 0 if side == 0 else cy - 1
            at = YB if side == 0 else YB + ty * (edge % 3) + ty - 8
            for i in range(-1, 4):
                lo, hi, dst = y_windows[i]
                child = 3 * (a - fx) + i
                on = (b == fy + edge // 3) & (a >= fx) & (child >= 0) & (child < cx)
                yield on, pltpu.make_async_remote_copy(
                    src_ref=S.at[:, pl.ds(XB + lo, hi - lo), pl.ds(at, 8), :],
                    dst_ref=ystrip.at[:, pl.ds(dst, hi - lo), :, :],
                    send_sem=strip_send.at[1, side, i + 1], recv_sem=strip_recv.at[1, kinds[i]],
                    device_id=(1, child, edge), device_id_type=MESH,
                )

    def strip_wait(axis, kind, lo, hi, dst):
        if axis == 0:
            ref = xstrip.at[:, :, pl.ds(dst, hi - lo), :]
        else:
            ref = ystrip.at[:, pl.ds(dst, hi - lo), :, :]
        pltpu.make_async_remote_copy(
            src_ref=ref, dst_ref=ref, send_sem=strip_send.at[0, 0, 0],
            recv_sem=strip_recv.at[axis, kind], device_id=(g, a, b), device_id_type=MESH,
        ).wait_recv()

    def wait_strips(axis, place, count, windows):
        for i in range(3):
            @pl.when(place % 3 == i)
            def _():
                strip_wait(axis, 0, *windows[i])

        @pl.when((place % 3 == 2) & (place < count - 1))
        def _():
            strip_wait(axis, 1, *windows[-1])

        @pl.when((place % 3 == 0) & (place > 0))
        def _():
            strip_wait(axis, 2, *windows[3])

    def relax_at(x, y):
        gx, gy = a * nx + x, b * ny + y
        depth = jnp.minimum(
            jnp.minimum(gx, nx * cx - 1 - gx), jnp.minimum(gy, ny * cy - 1 - gy)
        ).astype(F32)
        return jnp.maximum(1.0 - depth / BAND, 0.0)

    def y_edge(col):
        def row(u, _):
            n = lax.broadcasted_iota(jnp.int32, (24, lev), 0)
            relax = relax_at(3 * u + (n >> 3), col + (n & 7))
            w_high, w_low = split(wy[pl.ds(3 * u, 3)].reshape(24, 24))
            for c in range(3):
                s_high, s_low = split(ystrip[c, pl.ds(u, 3)].reshape(24, lev))
                bound = dot(w_high, s_high) + (dot(w_low, s_high) + dot(w_high, s_low))
                at = (c, pl.ds(XB + 3 * u, 3), pl.ds(YB + col, 8), slice(None))
                now = S[at].reshape(24, lev)
                S[at] = (now + relax * (bound - now)).reshape(3, 8, lev)
            return 0

        lax.fori_loop(0, tx, row, 0)

    def x_edge(first):
        def row(i, _):
            x = first + i
            w_high, w_low = split(wx[i])
            relax = relax_at(x, lax.broadcasted_iota(jnp.int32, (ny, lev), 0))
            for c in range(3):
                s_high, s_low = split(xstrip[c].reshape(3 * (ty + 16), lev))
                bound = dot(w_high, s_high) + (dot(w_low, s_high) + dot(w_high, s_low))
                now = mean[c, i]
                S[c, XB + x, YB : YB + ny, :] = now + relax * (bound - now)
            return 0

        lax.fori_loop(0, BAND, row, 0)

    @pl.when(g == 1)
    def _():
        restrict((0,))
        fb_start(0)
        pass_on()
        x_low, x_high = a == 0, a == cx - 1
        y_low, y_high = b == 0, b == cy - 1

        @pl.when(x_low)
        def _():
            for c in range(3):
                mean[c, 0:BAND] = S[c, XB : XB + BAND, YB : YB + ny, :]

        @pl.when(x_high)
        def _():
            for c in range(3):
                mean[c, 0:BAND] = S[c, XB + nx - BAND : XB + nx, YB : YB + ny, :]

        @pl.when(x_low | x_high)
        def _():
            xstrip_pad = jnp.zeros((3, 3, 8, lev), F32)

            @pl.when(y_low)
            def _():
                xstrip[:, :, 0:8, :] = xstrip_pad

            if (cy - 1) % 3 == 2:

                @pl.when(y_high)
                def _():
                    xstrip[:, :, ty + 8 : ty + 16, :] = xstrip_pad

        @pl.when(y_low | y_high)
        def _():
            @pl.when(x_low)
            def _():
                ystrip[:, 0:1] = jnp.zeros((3, 1, 8, lev), F32)

            if (cx - 1) % 3 == 2:

                @pl.when(x_high)
                def _():
                    ystrip[:, tx + 1 : tx + 2] = jnp.zeros((3, 1, 8, lev), F32)

            wait_strips(1, a, cx, y_windows)

        @pl.when(y_low)
        def _():
            y_edge(0)

        @pl.when(y_high)
        def _():
            y_edge(ny - 8)

        @pl.when(x_low | x_high)
        def _():
            wait_strips(0, b, cy, x_windows)

        @pl.when(x_low)
        def _():
            x_edge(0)

        @pl.when(x_high)
        def _():
            x_edge(nx - BAND)

        for c in range(3):
            hop(rst.at[c], rst.at[c], (g, a, b), fb_send.at[c], q_recv.at[0, c]).wait_send()

    @pl.when(g == 0)
    def _():
        for on, copy in strip_copies():
            @pl.when(on)
            def _():
                copy.start()
        pass_on()
        for on, copy in strip_copies():
            @pl.when(on)
            def _():
                copy.wait_send()
        for i in range(3):
            for j in range(3):
                there = (
                    (a >= fx) & (b >= fy) & (3 * (a - fx) + i < cx) & (3 * (b - fy) + j < cy)
                )

                @pl.when(there)
                def _():
                    for c in (1, 2, 0):
                        piece = fb.at[3 * i + j, c]
                        pltpu.make_async_remote_copy(
                            src_ref=piece, dst_ref=piece, send_sem=fb_send.at[c],
                            recv_sem=fb_recv.at[3 * i + j, c], device_id=(g, a, b),
                            device_id_type=MESH,
                        ).wait_recv()
                        at = (c, slice(XB + i * tx, XB + (i + 1) * tx),
                              slice(YB + j * ty, YB + (j + 1) * ty), slice(None))
                        now = S[at]
                        S[at] = now + FEEDBACK * (piece[...] - now)

    for k in range(SUBS):
        for d in range(4):
            @pl.when(dirs[d][0])
            def _():
                halo_copy(k, d).wait_send()
    passed_on()


def per_device(
    state, courant, vert_inverse, interp_index, interp_weight, restrict_index, restrict_weight
):
    cx, cy = lax.axis_size("gx"), lax.axis_size("gy")
    _, _, nx, ny, lev = state.shape
    tx, ty = nx // 3, ny // 3
    vmem = lambda *shape: pltpu.VMEM(shape, F32)
    dma = pltpu.SemaphoreType.DMA
    anywhere = pl.BlockSpec(memory_space=pltpu.HBM)
    inside = pl.BlockSpec(memory_space=pltpu.VMEM)
    padded = pl.pallas_call(
        functools.partial(kernel, cx, cy),
        out_shape=vmem(3, nx + 4, ny + 16, lev),
        in_specs=[anywhere] * 7,
        out_specs=inside,
        scratch_shapes=[
            vmem(nx + 2, ny + 16, lev),
            vmem(lev, 1, lev),
            pltpu.VMEM((nx, 4, ny), jnp.int32),
            vmem(nx, 4, ny),
            pltpu.VMEM((9, tx, ty), jnp.int32),
            vmem(9, tx, ty),
            vmem(3, nx, ny, lev),
            vmem(tx, ty, 3 * ny),
            vmem(BAND, ny, 3 * (ty + 16)),
            vmem(nx, 8, 24),
            vmem(2, 4, ny, lev),
            vmem(2, nx, 4, lev),
            vmem(2, 4, ny, lev),
            vmem(2, nx, 4, lev),
            vmem(SUBS - 1, 2, 2, ny, lev),
            vmem(SUBS - 1, 2, nx, 2, lev),
            vmem(SUBS - 1, 2, 2, ny, lev),
            vmem(SUBS - 1, 2, nx, 2, lev),
            vmem(3, tx, ty, lev),
            vmem(9, 3, tx, ty, lev),
            vmem(3, 3, ty + 16, lev),
            vmem(3, tx + 2, 8, lev),
            dma((7,)),
            dma((SUBS, 4)),
            dma((SUBS, 4)),
            dma((2, 2, 5)),
            dma((2, 3)),
            dma((3,)),
            dma((9, 3)),
            vmem(3, tx, ty, lev),
            vmem(3, tx, ty, lev),
            vmem(3, 3, tx, ty, lev),
            vmem(3, tx, ty, lev),
            dma((6, 3)),
            dma((6, 3)),
        ],
        compiler_params=pltpu.CompilerParams(
            has_side_effects=True, collective_id=0, vmem_limit_bytes=67043328 - 4 * (3 * (nx + 4) * (ny + 16) * 128) - 2**14
        ),
        name="nest_step",
    )(
        state, courant, vert_inverse.transpose(1, 0, 2),
        interp_index.transpose(0, 2, 1), interp_weight.transpose(0, 2, 1),
        restrict_index.transpose(2, 0, 1), restrict_weight.transpose(2, 0, 1),
    )
    return padded[None, :, XB : XB + nx, YB : YB + ny, :]


def solution(mesh):
    return jax.shard_map(
        per_device,
        mesh=mesh,
        in_specs=(
            P("grp", None, "gx", "gy", None),
            P("grp", "gx", "gy", None),
            P("grp", None, None),
            P("gx", "gy", None),
            P("gx", "gy", None),
            P("gx", "gy", None),
            P("gx", "gy", None),
        ),
        out_specs=P("grp", None, "gx", "gy", None),
        check_vma=False,
    )
```

profile of v0, /device:TPU:20, one launch (start us, length us, event | category | flops | bytes accessed | tf_op | source)
XLA Modules:
  0.0 51.7 jit_solution(9315877748816676614)
XLA Ops:
  0.0 49.9 %nest_step.1 = f32[3,40,64,90]{3,2,1,0:T(8,128)S(1)} custom-call(f32[1,3,36,48,90]{4,3,2,1,0:T(8,128)} %state.1, f32[1,36,48,90]{3,2,1,0:T(8,128)} %courant.1, f32[90,1,90]{2,1,0:T(1,128)} %bitcast.11, s32[36,4,48]{2,1,0:T(4,128)} %bitcast.7, f32[36,4,48]{2,1,0:T(4,128)} %bitcast.8, s32[9,12,16]{2,1,0:T(8,128)} %bitcast.9, f32[9,12,16]{2,1,0:T(8,128)} %bitcast.10), custom_call_target="tpu_custom_call" | custom-call | tf_op jit(solution)/shard_map/nest_step/pallas_call | solution.py:671
  49.9 1.7 %slice_bitcast_fusion = f32[1,3,36,48,90]{4,3,2,1,0:T(8,128)} fusion(f32[3,40,64,90]{3,2,1,0:T(8,128)S(1)} %nest_step.1), kind=kLoop, calls=%fused_computation | loop fusion | bytes 3732480 | tf_op jit(solution)/shard_map/broadcast_in_dim | solution.py:722
where the time goes:
time: 51.8 us; the launch traced here: 51.7 us
  Pallas kernels  49.9 us (96%)
  local copies, waits for them, and re-layouts  1.73 us (3%)
    pallas_call x1, Pallas kernels, per_device(): pl.pallas_call(functools.partial(kernel, cx, cy), out_shape=vmem(3, nx +...  49.9 us
    broadcast_in_dim x1, local copies, waits for them, and re-layouts, per_device(): return padded[None, :, XB:XB + nx, YB:YB + ny, :]  1.73 us

commit v1 on v0

--- a/solution.py
+++ b/solution.py
@@ -31,14 +31,6 @@
 
 def third(t):
     return (t * 11) >> 5
-
-
-def dense(cells, shares, depth):
-    places = lax.broadcasted_iota(jnp.int32, (depth, cells[0].shape[1]), 0)
-    total = jnp.zeros(places.shape, F32)
-    for cell, share in zip(cells, shares):
-        total = total + jnp.where(places == cell, share, 0.0)
-    return total.T
 
 
 def kernel(
@@ -216,7 +208,11 @@
         if k == 0:
             @pl.when(g == 1)
             def _():
-                weights()
+                restrict_weights()
+        if k == 1:
+            @pl.when((g == 1) & ((a == 0) | (a == cx - 1) | (b == 0) | (b == cy - 1)))
+            def _():
+                boundary_weights()
         for d in range(4):
             @pl.when(dirs[d][1])
             def _():
@@ -356,95 +352,82 @@
                     hop(buffer, buffer, (g, a, b), q_send.at[n, c], q_recv.at[n, c]).wait_send()
 
     def restrict(comps):
-        group = 4
-
-        def rows(i, _):
+        def rows(u, _):
             new = []
-            for j in range(group):
-                u = i * group + j
-                w_high, w_low = split(wr[u])
-                for c in comps:
-                    block = mean[c, pl.ds(3 * u, 3)].reshape(3 * ny, lev)
-                    b_high, b_low = split(block)
-                    both = dot(w_high, b_high) + (dot(w_low, b_high) + dot(w_high, b_low))
-                    new.append((c, u, both))
-            for c, u, both in new:
-                rst[c, u] = both
+            for c in comps:
+                total = None
+                for t in range(9):
+                    part = wr[u, t] * mean[c, 3 * u + t // 3, pl.ds(t % 3, ty, stride=3), :]
+                    total = part if total is None else total + part
+                new.append((c, total))
+            for c, total in new:
+                rst[c, u] = total
             return 0
 
-        lax.fori_loop(0, tx // group, rows, 0)
+        lax.fori_loop(0, tx, rows, 0)
+
+    def restrict_weights():
+        terms = range(ridx.shape[0])
+        w = [rwgt[k] for k in terms]
+        scale = (1.0 / SUBS) / row_sum(w)
+        shares = [part * scale for part in w]
+        index = [ridx[k] for k in terms]
+        for t in range(9):
+            at = row_sum([jnp.where(index[k] == t, shares[k], 0.0) for k in terms]).T
+            for u in range(tx):
+                wr[u, t] = jnp.broadcast_to(at[:, u : u + 1], (ty, lev))
+
+    def boundary_weights():
+        share = iwgt[...] / jnp.sum(iwgt[...], axis=1, keepdims=True)
+        share = share.reshape(nx * 4, ny).T
+        index = iidx[...].astype(F32).reshape(nx * 4, ny).T.astype(jnp.int32)
+        over = third(index)
+        shape = index.shape
+        x3 = (lax.broadcasted_iota(jnp.int32, shape, 1) * 171) >> 11
+        y3 = (lax.broadcasted_iota(jnp.int32, shape, 0) * 171) >> 9
+        source_x = jnp.clip(a * tx + x3 + over - 1, 0, cx * tx - 1)
+        source_y = jnp.clip(b * ty + y3 + (index - 3 * over) - 1, 0, cy * ty - 1)
+
+        def spread(cells, parts, x, depth):
+            places = lax.broadcasted_iota(jnp.int32, (cells.shape[0], depth), 1)
+            total = jnp.zeros(places.shape, F32)
+            for n in range(4 * x, 4 * x + 4):
+                total = total + jnp.where(places == cells[:, n : n + 1], parts[:, n : n + 1], 0.0)
+            return total
+
+        def y_weights(col, strip0):
+            cells = (source_x - (a * tx - 1)) * 8 + source_y - (b * ty + strip0)
+            cells, parts = cells[col : col + 8], share[col : col + 8]
+            for x in range(nx):
+                wy[8 * x : 8 * x + 8] = spread(cells, parts, x, 8 * (tx + 2))
+
+        def x_weights(first, strip0):
+            wide = ty + 16
+            cells = (source_x - (a * tx + strip0)) * wide + source_y - (b * ty - 8)
+            for i in range(BAND):
+                wx[ny * i : ny * i + ny] = spread(cells, share, first + i, 3 * wide)
+
+        @pl.when(b == 0)
+        def _():
+            y_weights(0, 0)
+
+        @pl.when(b == cy - 1)
+        def _():
+            y_weights(ny - 8, ty - 8)
+
+        @pl.when(a == 0)
+        def _():
+            x_weights(0, 0)
+
+        @pl.when(a == cx - 1)
+        def _():
+            x_weights(nx - BAND, tx - 3)
 
     def row_sum(rows):
         total = rows[0]
         for row in rows[1:]:
             total = total + row
         return total
-
-    def weights():
-        x_low, x_high = a == 0, a == cx - 1
-        y_low, y_high = b == 0, b == cy - 1
-
-        def restrict_row(u, _):
-            terms = range(ridx.shape[0])
-            w = [rwgt[k, pl.ds(u, 1), :] for k in terms]
-            scale = (1.0 / SUBS) / row_sum(w)
-            over = [third(ridx[k, pl.ds(u, 1), :]) for k in terms]
-            v3 = 3 * lax.broadcasted_iota(jnp.int32, (1, ty), 1)
-            cells = [
-                over[k] * (ny - 3) + ridx[k, pl.ds(u, 1), :] + v3 for k in terms
-            ]
-            wr[u] = dense(cells, [part * scale for part in w], 3 * ny)
-            return 0
-
-        lax.fori_loop(0, tx, restrict_row, 0)
-
-        def boundary_row(x, cols, origin_x, origin_y, width, depth):
-            w = [iwgt[x, k : k + 1, cols] for k in range(4)]
-            scale = 1.0 / row_sum(w)
-            y = cols.start + lax.broadcasted_iota(jnp.int32, w[0].shape, 1)
-            y3 = (y * 171) >> 9
-            cells = []
-            for k in range(4):
-                t = iidx[x, k : k + 1, cols]
-                over = third(t)
-                source_x = jnp.clip(a * tx + x // 3 + over - 1, 0, cx * tx - 1) - origin_x
-                source_y = jnp.clip(b * ty + y3 + (t - 3 * over) - 1, 0, cy * ty - 1) - origin_y
-                cells.append(source_x * width + source_y)
-            return dense(cells, [part * scale for part in w], depth)
-
-        def y_weights(col, strip0):
-            def row(x, _):
-                wy[x] = boundary_row(
-                    x, slice(col, col + 8), a * tx + x // 3 - 1, b * ty + strip0, 8, 24
-                )
-                return 0
-
-            lax.fori_loop(0, nx, row, 0)
-
-        def x_weights(first, strip0):
-            def row(i, _):
-                wx[i] = boundary_row(
-                    first + i, slice(0, ny), a * tx + strip0, b * ty - 8, ty + 16, 3 * (ty + 16)
-                )
-                return 0
-
-            lax.fori_loop(0, BAND, row, 0)
-
-        @pl.when(y_low)
-        def _():
-            y_weights(0, 0)
-
-        @pl.when(y_high)
-        def _():
-            y_weights(ny - 8, ty - 8)
-
-        @pl.when(x_low)
-        def _():
-            x_weights(0, 0)
-
-        @pl.when(x_high)
-        def _():
-            x_weights(nx - BAND, tx - 3)
 
     for k in range(SUBS):
         exchange(k)
@@ -521,34 +504,31 @@
         ).astype(F32)
         return jnp.maximum(1.0 - depth / BAND, 0.0)
 
+    def mixed(weights, source):
+        w_high, w_low = split(weights)
+        s_high, s_low = split(source)
+        return dot(w_high, s_high) + (dot(w_low, s_high) + dot(w_high, s_low))
+
     def y_edge(col):
-        def row(u, _):
-            n = lax.broadcasted_iota(jnp.int32, (24, lev), 0)
-            relax = relax_at(3 * u + (n >> 3), col + (n & 7))
-            w_high, w_low = split(wy[pl.ds(3 * u, 3)].reshape(24, 24))
-            for c in range(3):
-                s_high, s_low = split(ystrip[c, pl.ds(u, 3)].reshape(24, lev))
-                bound = dot(w_high, s_high) + (dot(w_low, s_high) + dot(w_high, s_low))
-                at = (c, pl.ds(XB + 3 * u, 3), pl.ds(YB + col, 8), slice(None))
-                now = S[at].reshape(24, lev)
-                S[at] = (now + relax * (bound - now)).reshape(3, 8, lev)
-            return 0
-
-        lax.fori_loop(0, tx, row, 0)
+        shape = (nx, 8, lev)
+        relax = relax_at(
+            lax.broadcasted_iota(jnp.int32, shape, 0), col + lax.broadcasted_iota(jnp.int32, shape, 1)
+        )
+        for c in range(3):
+            bound = mixed(wy[...], ystrip[c].reshape(8 * (tx + 2), lev)).reshape(shape)
+            at = (c, slice(XB, XB + nx), slice(YB + col, YB + col + 8), slice(None))
+            now = S[at]
+            S[at] = now + relax * (bound - now)
 
     def x_edge(first):
-        def row(i, _):
-            x = first + i
-            w_high, w_low = split(wx[i])
-            relax = relax_at(x, lax.broadcasted_iota(jnp.int32, (ny, lev), 0))
-            for c in range(3):
-                s_high, s_low = split(xstrip[c].reshape(3 * (ty + 16), lev))
-                bound = dot(w_high, s_high) + (dot(w_low, s_high) + dot(w_high, s_low))
-                now = mean[c, i]
-                S[c, XB + x, YB : YB + ny, :] = now + relax * (bound - now)
-            return 0
-
-        lax.fori_loop(0, BAND, row, 0)
+        shape = (BAND, ny, lev)
+        relax = relax_at(
+            first + lax.broadcasted_iota(jnp.int32, shape, 0), lax.broadcasted_iota(jnp.int32, shape, 1)
+        )
+        for c in range(3):
+            bound = mixed(wx[...], xstrip[c].reshape(3 * (ty + 16), lev)).reshape(shape)
+            now = mean[c, 0:BAND]
+            S[c, XB + first : XB + first + BAND, YB : YB + ny, :] = now + relax * (bound - now)
 
     @pl.when(g == 1)
     def _():
@@ -681,9 +661,9 @@
             pltpu.VMEM((9, tx, ty), jnp.int32),
             vmem(9, tx, ty),
             vmem(3, nx, ny, lev),
-            vmem(tx, ty, 3 * ny),
-            vmem(BAND, ny, 3 * (ty + 16)),
-            vmem(nx, 8, 24),
+            vmem(tx, 9, ty, lev),
+            vmem(BAND * ny, 3 * (ty + 16)),
+            vmem(nx * 8, 8 * (tx + 2)),
             vmem(2, 4, ny, lev),
             vmem(2, nx, 4, lev),
             vmem(2, 4, ny, lev),

time: 51.8 us -> 45.8 us (0.88)
  Pallas kernels: 49.9 us -> 44 us
    pallas_call x1, Pallas kernels: 49.9 us -> 44 us  [per_device(): pl.pallas_call(functools.partial(kernel, cx, cy), out_shape=vmem(3, nx +...]
where the time goes in v1:
time: 45.8 us; the launch traced here: 45.7 us
  Pallas kernels  44 us (96%)
  local copies, waits for them, and re-layouts  1.73 us (4%)
    pallas_call x1, Pallas kernels, per_device(): pl.pallas_call(functools.partial(kernel, cx, cy), out_shape=vmem(3, nx +...  44 us
    broadcast_in_dim x1, local copies, waits for them, and re-layouts, per_device(): return padded[None, :, XB:XB + nx, YB:YB + ny, :]  1.73 us

profile of v1, /device:TPU:20, one launch (start us, length us, event | category | flops | bytes accessed | tf_op | source)
XLA Modules:
  0.0 45.7 jit_solution(15891225303645558444)
XLA Ops:
  0.0 44.0 %nest_step.1 = f32[3,40,64,90]{3,2,1,0:T(8,128)S(1)} custom-call(f32[1,3,36,48,90]{4,3,2,1,0:T(8,128)} %state.1, f32[1,36,48,90]{3,2,1,0:T(8,128)} %courant.1, f32[90,1,90]{2,1,0:T(1,128)} %bitcast.11, s32[36,4,48]{2,1,0:T(4,128)} %bitcast.7, f32[36,4,48]{2,1,0:T(4,128)} %bitcast.8, s32[9,12,16]{2,1,0:T(8,128)} %bitcast.9, f32[9,12,16]{2,1,0:T(8,128)} %bitcast.10), custom_call_target="tpu_custom_call" | custom-call | tf_op jit(solution)/shard_map/nest_step/pallas_call | solution.py:651
  44.0 1.7 %slice_bitcast_fusion = f32[1,3,36,48,90]{4,3,2,1,0:T(8,128)} fusion(f32[3,40,64,90]{3,2,1,0:T(8,128)S(1)} %nest_step.1), kind=kLoop, calls=%fused_computation | loop fusion | bytes 3732480 | tf_op jit(solution)/shard_map/broadcast_in_dim | solution.py:702

commit v2 on v1

--- a/solution.py
+++ b/solution.py
@@ -41,12 +41,13 @@
     S,
     C, inverse, iidx, iwgt, ridx, rwgt, mean, wr, wx, wy, sx0, sy0, rx0, ry0, sx, sy, rx, ry, rst, fb, xstrip, ystrip,
     load_sem, halo_send, halo_recv, strip_send, strip_recv, fb_send, fb_recv,
-    q0, q1, q2, q3, q_send, q_recv,
+    q0, q1, q2, xpack, ypack, q_send, q_recv,
     ) = rest[:5], rest[5:]
     g, a, b = lax.axis_index("grp"), lax.axis_index("gx"), lax.axis_index("gy")
     nx, ny, lev = state.shape[2], state.shape[3], state.shape[4]
     tx, ty = nx // 3, ny // 3
     fx, fy = cx // 2, cy // 2
+    quarter, slot = tx // 4, lev // 3
 
     barrier = pltpu.get_barrier_semaphore()
     greeted = []
@@ -87,23 +88,21 @@
         to_a, to_b = fx + at_a // 3, fy + at_b // 3
         far = (at_a != to_a) & (at_b != to_b)
         direct = (at_a == to_a) & (at_b == to_b)
-        by_nest = (at_a % 3 == 1) & (at_b == to_b) & (at_a != to_a)
-        over = jnp.logical_not(direct | by_nest)
+        over = jnp.logical_not(direct)
         along_a = over & (at_a % 3 == 1) & far
         along_b = over & (at_a % 3 == 0) & far
         last = over & jnp.logical_not(along_a | along_b)
-        return to_a, to_b, direct, by_nest, over, along_a, along_b, last
-
-    to_a, to_b, direct, by_nest, over, along_a, along_b, last = route(a, b)
+        return to_a, to_b, direct, over, along_a, along_b, last
+
+    to_a, to_b, direct, over, along_a, along_b, last = route(a, b)
     parent, nest = g == 0, g == 1
     mid_a = 3 * (a - fx) + 1
     comes = (a >= fx) & (mid_a < cx)
-    middle = route(mid_a, b)
-    relay1, relay3 = parent & comes & middle[5], nest & comes & middle[3]
+    relay1 = parent & comes & route(mid_a, b)[4]
     relay2 = []
     for j in range(3):
         side_b = 3 * (b - fy) + j
-        relay2.append((parent & (b >= fy) & (side_b < cy) & route(a, side_b)[6], side_b))
+        relay2.append((parent & (b >= fy) & (side_b < cy) & route(a, side_b)[5], side_b))
     greet(nest & over, (0, a, b))
     greet(parent & over, (1, a, b))
     greet(parent & along_a, (0, to_a, b))
@@ -112,19 +111,13 @@
     for on, side_b in relay2:
         greet(on, (0, a, side_b))
         greet(on, (0, to_a, b))
-    greet(nest & by_nest, (1, to_a, b))
-    greet(relay3, (1, mid_a, b))
     greet(parent & last, (0, to_a, to_b))
     greet(relay1, (0, a, to_b))
-    greet(relay3, (0, a, b))
-    greet(nest & direct, (0, a, b))
     for i in range(3):
         for j in range(3):
             from_a, from_b = 3 * (a - fx) + i, 3 * (b - fy) + j
             on = parent & (a >= fx) & (b >= fy) & (from_a < cx) & (from_b < cy)
-            _, _, f_direct, f_nest, _, f_a, f_b, f_last = route(from_a, from_b)
-            greet(on & f_direct, (1, a, b))
-            greet(on & f_nest, (1, a, from_b))
+            f_a, f_b, f_last = route(from_a, from_b)[4:]
             greet(on & f_a, (0, a, from_b))
             greet(on & f_b, (0, from_a, b))
             greet(on & f_last, (0, from_a, from_b))
@@ -154,10 +147,12 @@
         S[c, XB : XB + nx, YB + ny : YB + ny + 8, :] = zcol
     C[1 : 1 + nx, 0:YB, :] = zcol
     C[1 : 1 + nx, YB + ny : YB + ny + 8, :] = zcol
-    for copy in loads:
-        copy.wait()
+    with jax.named_scope("loads"):
+        for copy in loads:
+            copy.wait()
     m_high, m_low = split(inverse[:, 0, :])
-    pl.semaphore_wait(barrier, sum(on.astype(jnp.int32) for on in greeted))
+    with jax.named_scope("greet"):
+        pl.semaphore_wait(barrier, sum(on.astype(jnp.int32) for on in greeted))
 
     dirs = (
         (a > 0, a < cx - 1, (g, a - 1, b)),
@@ -175,9 +170,15 @@
             src, dst = src.at[k - 1, d % 2], dst.at[k - 1, d % 2]
         return pltpu.make_async_remote_copy(
             src_ref=src, dst_ref=dst,
-            send_sem=halo_send.at[k, d], recv_sem=halo_recv.at[k, d],
+            send_sem=halo_send.at[d], recv_sem=halo_recv.at[k % 2, d],
             device_id=dirs[d][2], device_id_type=MESH,
         )
+
+    def halo_sent(k):
+        for d in range(4):
+            @pl.when(dirs[d][0])
+            def _():
+                halo_copy(k, d).wait_send()
 
     def exchange(k):
         cols = slice(YB, YB + ny)
@@ -201,6 +202,8 @@
             sx[k - 1, 1] = S[0, last_x - 2 : last_x, cols, :]
             sy[k - 1, 0] = S[0, rows, YB : YB + 2, :]
             sy[k - 1, 1] = S[0, rows, last_y - 2 : last_y, :]
+        if k > 0:
+            halo_sent(k - 1)
         for d in range(4):
             @pl.when(dirs[d][0])
             def _():
@@ -208,11 +211,13 @@
         if k == 0:
             @pl.when(g == 1)
             def _():
-                restrict_weights()
+                with jax.named_scope("restrict_weights"):
+                    restrict_weights()
         if k == 1:
             @pl.when((g == 1) & ((a == 0) | (a == cx - 1) | (b == 0) | (b == cy - 1)))
             def _():
-                boundary_weights()
+                with jax.named_scope("boundary_weights"):
+                    boundary_weights()
         for d in range(4):
             @pl.when(dirs[d][1])
             def _():
@@ -298,14 +303,16 @@
 
     def home(src, c, i, j, device, send):
         n = 3 * i + j
-        return hop(src, fb.at[n, c], device, send, fb_recv.at[n, c])
+        return hop(src, fb.at[n, c], device, send, fb_recv.at[n, min(c, 1)])
 
     def fb_copies(c):
-        mine, sem = rst.at[c], fb_send.at[c]
+        mine, sem = rst.at[c], fb_send.at[min(c, 1)]
+        straight = home(mine, c, a % 3, b % 3, (0, to_a, to_b), sem)
+        if c == 0:
+            return ((nest, straight),)
         return (
-            (direct, home(mine, c, a % 3, b % 3, (0, a, b), sem)),
-            (by_nest, hop(mine, q3.at[c], (1, to_a, b), sem, q_recv.at[5, c])),
-            (over, hop(mine, q0.at[c], (0, a, b), sem, q_recv.at[0, c])),
+            (direct, straight),
+            (over, hop(mine, q0.at[c - 1], (0, a, b), sem, q_recv.at[0, c - 1])),
         )
 
     def fb_start(c):
@@ -315,56 +322,60 @@
                 copy.start()
 
     def relays(c):
-        sem0 = q_send.at[0, c]
-        yield parent & over, q0.at[c], 0, (
-            (along_a, hop(q0.at[c], q1.at[c], (0, to_a, b), sem0, q_recv.at[1, c])),
-            (along_b, hop(q0.at[c], q2.at[b % 3, c], (0, a, to_b), sem0,
-                          q_recv.at[2 + b % 3, c])),
-            (last, home(q0.at[c], c, a % 3, b % 3, (0, to_a, to_b), sem0)),
+        n = c - 1
+        sem0 = q_send.at[0]
+        yield parent & over, q0, 0, (
+            (along_a, hop(q0.at[n], q1.at[n], (0, to_a, b), sem0, q_recv.at[1, n])),
+            (along_b, hop(q0.at[n], q2.at[b % 3, n], (0, a, to_b), sem0,
+                          q_recv.at[2 + b % 3, n])),
+            (last, home(q0.at[n], c, a % 3, b % 3, (0, to_a, to_b), sem0)),
         )
-        yield relay1, q1.at[c], 1, (
-            (relay1, home(q1.at[c], c, 1, b % 3, (0, a, to_b), q_send.at[1, c])),
+        yield relay1, q1, 1, (
+            (relay1, home(q1.at[n], c, 1, b % 3, (0, a, to_b), q_send.at[1])),
         )
         for j, (on, side_b) in enumerate(relay2):
-            yield on, q2.at[j, c], 2 + j, (
-                (on, home(q2.at[j, c], c, 0, j, (0, to_a, b), q_send.at[2 + j, c])),
+            yield on, q2.at[j], 2 + j, (
+                (on, home(q2.at[j, n], c, 0, j, (0, to_a, b), q_send.at[2 + j])),
             )
-        yield relay3, q3.at[c], 5, (
-            (relay3, home(q3.at[c], c, 1, b % 3, (0, a, b), q_send.at[5, c])),
-        )
 
     def pass_on():
-        for c in (1, 2, 0):
-            for here, buffer, n, onward in relays(c):
+        for stages in zip(relays(1), relays(2)):
+            for n, (here, buffer, stage, onward) in enumerate(stages):
                 @pl.when(here)
                 def _():
-                    hop(buffer, buffer, (g, a, b), q_send.at[n, c], q_recv.at[n, c]).wait_recv()
+                    piece = buffer.at[n]
+                    hop(piece, piece, (g, a, b), q_send.at[stage], q_recv.at[stage, n]).wait_recv()
                     for on, copy in onward:
                         @pl.when(on)
                         def _():
                             copy.start()
 
     def passed_on():
-        for c in (1, 2, 0):
-            for here, buffer, n, onward in relays(c):
-                @pl.when(here)
-                def _():
-                    hop(buffer, buffer, (g, a, b), q_send.at[n, c], q_recv.at[n, c]).wait_send()
+        for here, buffer, stage, _ in relays(1):
+            @pl.when(here)
+            def _():
+                hop(buffer, buffer, (g, a, b), q_send.at[stage], q_recv.at[0, 0]).wait_send()
 
     def restrict(comps):
-        def rows(u, _):
+        def mixed_row(c, u):
+            total = None
+            for t in range(9):
+                part = wr[u, t] * mean[c, 3 * u + t // 3, pl.ds(t % 3, ty, stride=3), :]
+                total = part if total is None else total + part
+            return total
+
+        def rows(i, _):
             new = []
+            spare = jnp.zeros((ty, 128 - lev - slot), F32)
             for c in comps:
-                total = None
-                for t in range(9):
-                    part = wr[u, t] * mean[c, 3 * u + t // 3, pl.ds(t % 3, ty, stride=3), :]
-                    total = part if total is None else total + part
-                new.append((c, total))
-            for c, total in new:
-                rst[c, u] = total
+                guest = mixed_row(c, 3 * quarter + i)
+                for m in range(3):
+                    new.append((c, 3 * i + m, mixed_row(c, 3 * i + m), guest[:, m * slot : (m + 1) * slot]))
+            for c, u, own, part in new:
+                rst[c, u] = jnp.concatenate([own, part, spare], axis=1)
             return 0
 
-        lax.fori_loop(0, tx, rows, 0)
+        lax.fori_loop(0, quarter, rows, 0)
 
     def restrict_weights():
         terms = range(ridx.shape[0])
@@ -396,10 +407,10 @@
             return total
 
         def y_weights(col, strip0):
-            cells = (source_x - (a * tx - 1)) * 8 + source_y - (b * ty + strip0)
+            cells = (source_x - (a * tx - 1)) * 4 + source_y - (b * ty + strip0)
             cells, parts = cells[col : col + 8], share[col : col + 8]
             for x in range(nx):
-                wy[8 * x : 8 * x + 8] = spread(cells, parts, x, 8 * (tx + 2))
+                wy[8 * x : 8 * x + 8] = spread(cells, parts, x, 4 * (tx + 2))
 
         def x_weights(first, strip0):
             wide = ty + 16
@@ -413,7 +424,7 @@
 
         @pl.when(b == cy - 1)
         def _():
-            y_weights(ny - 8, ty - 8)
+            y_weights(ny - 8, ty - 4)
 
         @pl.when(a == 0)
         def _():
@@ -429,49 +440,72 @@
             total = total + row
         return total
 
-    for k in range(SUBS):
-        exchange(k)
-        winds(k)
-        if k == SUBS - 1:
-            @pl.when(g == 1)
-            def _():
-                restrict((1, 2))
-                fb_start(1)
-                fb_start(2)
-        press(k)
-
     x_windows = {-1: (0, 8, 24), 0: (0, ty + 8, 8), 1: (ty - 8, 2 * ty + 8, 0),
                  2: (2 * ty - 8, ny, 0), 3: (ny - 8, ny, 0)}
     y_windows = {-1: (0, 1, tx + 1), 0: (0, tx + 1, 1), 1: (tx - 1, 2 * tx + 1, 0),
                  2: (2 * tx - 1, nx, 0), 3: (nx - 1, nx, 0)}
     kinds = {-1: 1, 0: 0, 1: 0, 2: 0, 3: 2}
 
-    def strip_copies():
+    def x_side(side):
+        edge = 0 if side == 0 else cx - 1
+        at = XB if side == 0 else XB + tx * (edge % 3) + tx - 3
+        return edge, (a == fx + edge // 3) & (b >= fy), at
+
+    def y_side(side):
+        edge = 0 if side == 0 else cy - 1
+        at = YB if side == 0 else YB + ty * (edge % 3) + ty - 4
+        return edge, (b == fy + edge // 3) & (a >= fx), at
+
+    def strip_pack(comps):
         for side in range(2):
-            edge = 0 if side == 0 else cx - 1
-            at = XB if side == 0 else XB + tx * (edge % 3) + tx - 3
+            _, on, x_at = x_side(side)
+
+            @pl.when(on)
+            def _():
+                for c in comps:
+                    xpack[c] = S[c, x_at : x_at + 3, YB : YB + ny, :]
+
+            _, on, y_at = y_side(side)
+
+            @pl.when(on)
+            def _():
+                for c in comps:
+                    ypack[c] = S[c, XB : XB + nx, y_at : y_at + 4, :]
+
+    def strip_copies(comps):
+        for side in range(2):
+            edge, here, _ = x_side(side)
             for j in range(-1, 4):
                 lo, hi, dst = x_windows[j]
                 child = 3 * (b - fy) + j
-                on = (a == fx + edge // 3) & (b >= fy) & (child >= 0) & (child < cy)
-                yield on, pltpu.make_async_remote_copy(
-                    src_ref=S.at[:, pl.ds(at, 3), pl.ds(YB + lo, hi - lo), :],
-                    dst_ref=xstrip.at[:, :, pl.ds(dst, hi - lo), :],
-                    send_sem=strip_send.at[0, side, j + 1], recv_sem=strip_recv.at[0, kinds[j]],
+                yield here & (child >= 0) & (child < cy), pltpu.make_async_remote_copy(
+                    src_ref=xpack.at[comps, :, pl.ds(lo, hi - lo), :],
+                    dst_ref=xstrip.at[comps, :, pl.ds(dst, hi - lo), :],
+                    send_sem=strip_send.at[0, j + 1], recv_sem=strip_recv.at[0, kinds[j]],
                     device_id=(1, edge, child), device_id_type=MESH,
                 )
-            edge = 0 if side == 0 else cy - 1
-            at = YB if side == 0 else YB + ty * (edge % 3) + ty - 8
+            edge, here, _ = y_side(side)
             for i in range(-1, 4):
                 lo, hi, dst = y_windows[i]
                 child = 3 * (a - fx) + i
-                on = (b == fy + edge // 3) & (a >= fx) & (child >= 0) & (child < cx)
-                yield on, pltpu.make_async_remote_copy(
-                    src_ref=S.at[:, pl.ds(XB + lo, hi - lo), pl.ds(at, 8), :],
-                    dst_ref=ystrip.at[:, pl.ds(dst, hi - lo), :, :],
-                    send_sem=strip_send.at[1, side, i + 1], recv_sem=strip_recv.at[1, kinds[i]],
+                yield here & (child >= 0) & (child < cx), pltpu.make_async_remote_copy(
+                    src_ref=ypack.at[comps, pl.ds(lo, hi - lo)],
+                    dst_ref=ystrip.at[comps, pl.ds(dst, hi - lo)],
+                    send_sem=strip_send.at[1, i + 1], recv_sem=strip_recv.at[1, kinds[i]],
                     device_id=(1, child, edge), device_id_type=MESH,
                 )
+
+    def strip_start(comps):
+        for on, copy in strip_copies(comps):
+            @pl.when(on)
+            def _():
+                copy.start()
+
+    def strips_sent():
+        for on, copy in strip_copies(slice(0, 3)):
+            @pl.when(on)
+            def _():
+                copy.wait_send()
 
     def strip_wait(axis, kind, lo, hi, dst):
         if axis == 0:
@@ -479,7 +513,7 @@
         else:
             ref = ystrip.at[:, pl.ds(dst, hi - lo), :, :]
         pltpu.make_async_remote_copy(
-            src_ref=ref, dst_ref=ref, send_sem=strip_send.at[0, 0, 0],
+            src_ref=ref, dst_ref=ref, send_sem=strip_send.at[0, 0],
             recv_sem=strip_recv.at[axis, kind], device_id=(g, a, b), device_id_type=MESH,
         ).wait_recv()
 
@@ -515,7 +549,7 @@
             lax.broadcasted_iota(jnp.int32, shape, 0), col + lax.broadcasted_iota(jnp.int32, shape, 1)
         )
         for c in range(3):
-            bound = mixed(wy[...], ystrip[c].reshape(8 * (tx + 2), lev)).reshape(shape)
+            bound = mixed(wy[...], ystrip[c].reshape(4 * (tx + 2), lev)).reshape(shape)
             at = (c, slice(XB, XB + nx), slice(YB + col, YB + col + 8), slice(None))
             now = S[at]
             S[at] = now + relax * (bound - now)
@@ -530,11 +564,55 @@
             now = mean[c, 0:BAND]
             S[c, XB + first : XB + first + BAND, YB : YB + ny, :] = now + relax * (bound - now)
 
+    for k in range(SUBS):
+        with jax.named_scope(f"exchange{k}"):
+            exchange(k)
+        with jax.named_scope(f"winds{k}"):
+            winds(k)
+        if k == SUBS - 1:
+            @pl.when(g == 1)
+            def _():
+                with jax.named_scope("restrict_winds"):
+                    restrict((1, 2))
+                fb_start(1)
+                fb_start(2)
+
+            @pl.when(g == 0)
+            def _():
+                strip_pack((1, 2))
+                strip_start(slice(1, 3))
+        with jax.named_scope(f"press{k}"):
+            press(k)
+
+    def take(i, j, comps):
+        first, count = comps[0], len(comps)
+        with jax.named_scope(f"piece{i}{j}{first}"):
+            piece = fb.at[3 * i + j, first : first + count]
+            pltpu.make_async_remote_copy(
+                src_ref=piece, dst_ref=piece, send_sem=fb_send.at[0],
+                recv_sem=fb_recv.at[3 * i + j, min(first, 1)], device_id=(g, a, b),
+                device_id_type=MESH,
+            ).wait_recv()
+        for c in comps:
+            got = fb[3 * i + j, c]
+            parts = got.reshape(quarter, 3, ty, 128)[:, :, :, lev : lev + slot]
+            guest = jnp.concatenate([parts[:, m] for m in range(3)], axis=2)
+
+            def blend(u, count, value):
+                first = XB + i * tx + u
+                at = (c, slice(first, first + count), slice(YB + j * ty, YB + (j + 1) * ty), slice(None))
+                now = S[at]
+                S[at] = now + FEEDBACK * (value - now)
+
+            blend(0, 3 * quarter, got[:, :, :lev])
+            blend(3 * quarter, quarter, guest)
+
     @pl.when(g == 1)
     def _():
-        restrict((0,))
+        with jax.named_scope("restrict_pressure"):
+            restrict((0,))
         fb_start(0)
-        pass_on()
+        halo_sent(SUBS - 1)
         x_low, x_high = a == 0, a == cx - 1
         y_low, y_high = b == 0, b == cy - 1
 
@@ -566,76 +644,66 @@
         def _():
             @pl.when(x_low)
             def _():
-                ystrip[:, 0:1] = jnp.zeros((3, 1, 8, lev), F32)
+                ystrip[:, 0:1] = jnp.zeros((3, 1, 4, lev), F32)
 
             if (cx - 1) % 3 == 2:
 
                 @pl.when(x_high)
                 def _():
-                    ystrip[:, tx + 1 : tx + 2] = jnp.zeros((3, 1, 8, lev), F32)
-
-            wait_strips(1, a, cx, y_windows)
+                    ystrip[:, tx + 1 : tx + 2] = jnp.zeros((3, 1, 4, lev), F32)
+
+            with jax.named_scope("wait_y"):
+                wait_strips(1, a, cx, y_windows)
 
         @pl.when(y_low)
         def _():
-            y_edge(0)
+            with jax.named_scope("y_low"):
+                y_edge(0)
 
         @pl.when(y_high)
         def _():
-            y_edge(ny - 8)
+            with jax.named_scope("y_high"):
+                y_edge(ny - 8)
 
         @pl.when(x_low | x_high)
         def _():
-            wait_strips(0, b, cy, x_windows)
+            with jax.named_scope("wait_x"):
+                wait_strips(0, b, cy, x_windows)
 
         @pl.when(x_low)
         def _():
-            x_edge(0)
+            with jax.named_scope("x_low_edge"):
+                x_edge(0)
 
         @pl.when(x_high)
         def _():
-            x_edge(nx - BAND)
-
-        for c in range(3):
-            hop(rst.at[c], rst.at[c], (g, a, b), fb_send.at[c], q_recv.at[0, c]).wait_send()
+            with jax.named_scope("x_high_edge"):
+                x_edge(nx - BAND)
+
+        for part, comps in ((1, slice(1, 3)), (0, slice(0, 1))):
+            piece = rst.at[comps]
+            hop(piece, piece, (g, a, b), fb_send.at[part], q_recv.at[0, 0]).wait_send()
 
     @pl.when(g == 0)
     def _():
-        for on, copy in strip_copies():
-            @pl.when(on)
-            def _():
-                copy.start()
-        pass_on()
-        for on, copy in strip_copies():
-            @pl.when(on)
-            def _():
-                copy.wait_send()
-        for i in range(3):
-            for j in range(3):
-                there = (
-                    (a >= fx) & (b >= fy) & (3 * (a - fx) + i < cx) & (3 * (b - fy) + j < cy)
-                )
-
-                @pl.when(there)
-                def _():
-                    for c in (1, 2, 0):
-                        piece = fb.at[3 * i + j, c]
-                        pltpu.make_async_remote_copy(
-                            src_ref=piece, dst_ref=piece, send_sem=fb_send.at[c],
-                            recv_sem=fb_recv.at[3 * i + j, c], device_id=(g, a, b),
-                            device_id_type=MESH,
-                        ).wait_recv()
-                        at = (c, slice(XB + i * tx, XB + (i + 1) * tx),
-                              slice(YB + j * ty, YB + (j + 1) * ty), slice(None))
-                        now = S[at]
-                        S[at] = now + FEEDBACK * (piece[...] - now)
-
-    for k in range(SUBS):
-        for d in range(4):
-            @pl.when(dirs[d][0])
-            def _():
-                halo_copy(k, d).wait_send()
-    passed_on()
+        strip_pack((0,))
+        strip_start(slice(0, 1))
+        with jax.named_scope("pass_parent"):
+            pass_on()
+        halo_sent(SUBS - 1)
+        passed_on()
+        winds_of, pressure_of = (1, 2), (0,)
+        order = [((2, j), winds_of) for j in (2, 1, 0)] + [((2, j), pressure_of) for j in (2, 1, 0)]
+        order += [((1, 2), winds_of)] + [((i, j), pressure_of) for i in (1, 0) for j in (2, 1, 0)]
+        order += [(at, winds_of) for at in ((1, 1), (1, 0), (0, 2), (0, 1), (0, 0))]
+        for (i, j), comps in order:
+            there = (a >= fx) & (b >= fy) & (3 * (a - fx) + i < cx) & (3 * (b - fy) + j < cy)
+
+            @pl.when(there)
+            def _():
+                take(i, j, comps)
+
+        strips_sent()
 
 
 def per_device(
@@ -644,6 +712,7 @@
     cx, cy = lax.axis_size("gx"), lax.axis_size("gy")
     _, _, nx, ny, lev = state.shape
     tx, ty = nx // 3, ny // 3
+    packed = (3 * (tx // 4), ty, 128)
     vmem = lambda *shape: pltpu.VMEM(shape, F32)
     dma = pltpu.SemaphoreType.DMA
     anywhere = pl.BlockSpec(memory_space=pltpu.HBM)
@@ -663,7 +732,7 @@
             vmem(3, nx, ny, lev),
             vmem(tx, 9, ty, lev),
             vmem(BAND * ny, 3 * (ty + 16)),
-            vmem(nx * 8, 8 * (tx + 2)),
+            vmem(nx * 8, 4 * (tx + 2)),
             vmem(2, 4, ny, lev),
             vmem(2, nx, 4, lev),
             vmem(2, 4, ny, lev),
@@ -672,23 +741,24 @@
             vmem(SUBS - 1, 2, nx, 2, lev),
             vmem(SUBS - 1, 2, 2, ny, lev),
             vmem(SUBS - 1, 2, nx, 2, lev),
-            vmem(3, tx, ty, lev),
-            vmem(9, 3, tx, ty, lev),
+            vmem(3, *packed),
+            vmem(9, 3, *packed),
             vmem(3, 3, ty + 16, lev),
-            vmem(3, tx + 2, 8, lev),
+            vmem(3, tx + 2, 4, lev),
             dma((7,)),
-            dma((SUBS, 4)),
-            dma((SUBS, 4)),
-            dma((2, 2, 5)),
+            dma((4,)),
+            dma((2, 4)),
+            dma((2, 5)),
             dma((2, 3)),
-            dma((3,)),
-            dma((9, 3)),
-            vmem(3, tx, ty, lev),
-            vmem(3, tx, ty, lev),
-            vmem(3, 3, tx, ty, lev),
-            vmem(3, tx, ty, lev),
-            dma((6, 3)),
-            dma((6, 3)),
+            dma((2,)),
+            dma((9, 2)),
+            vmem(2, *packed),
+            vmem(2, *packed),
+            vmem(3, 2, *packed),
+            vmem(3, 3, ny, lev),
+            vmem(3, nx, 4, lev),
+            dma((5,)),
+            dma((5, 2)),
         ],
         compiler_params=pltpu.CompilerParams(
             has_side_effects=True, collective_id=0, vmem_limit_bytes=67043328 - 4 * (3 * (nx + 4) * (ny + 16) * 128) - 2**14

time: 45.8 us -> 40.8 us (0.89)
  Pallas kernels: 44 us -> 39 us
    pallas_call x1, Pallas kernels: 44 us -> 39 us  [per_device(): pl.pallas_call(functools.partial(kernel, cx, cy), out_shape=vmem(3, nx +...]
where the time goes in v2:
time: 40.8 us; the launch traced here: 40.7 us
  Pallas kernels  39 us (96%)
  local copies, waits for them, and re-layouts  1.73 us (4%)
    pallas_call x1, Pallas kernels, per_device(): pl.pallas_call(functools.partial(kernel, cx, cy), out_shape=vmem(3, nx +...  39 us
    broadcast_in_dim x1, local copies, waits for them, and re-layouts, per_device(): return padded[None, :, XB:XB + nx, YB:YB + ny, :]  1.73 us

profile of v2, /device:TPU:20, one launch (start us, length us, event | category | flops | bytes accessed | tf_op | source)
XLA Modules:
  0.0 40.7 jit_solution(15359323459508883978)
XLA Ops:
  0.0 39.0 %nest_step.1 = f32[3,40,64,90]{3,2,1,0:T(8,128)S(1)} custom-call(f32[1,3,36,48,90]{4,3,2,1,0:T(8,128)} %state.1, f32[1,36,48,90]{3,2,1,0:T(8,128)} %courant.1, f32[90,1,90]{2,1,0:T(1,128)} %bitcast.11, s32[36,4,48]{2,1,0:T(4,128)} %bitcast.7, f32[36,4,48]{2,1,0:T(4,128)} %bitcast.8, s32[9,12,16]{2,1,0:T(8,128)} %bitcast.9, f32[9,12,16]{2,1,0:T(8,128)} %bitcast.10), custom_call_target="tpu_custom_call" | custom-call | tf_op jit(solution)/shard_map/nest_step/pallas_call | solution.py:720
  39.0 1.7 %slice_bitcast_fusion = f32[1,3,36,48,90]{4,3,2,1,0:T(8,128)} fusion(f32[3,40,64,90]{3,2,1,0:T(8,128)S(1)} %nest_step.1), kind=kLoop, calls=%fused_computation | loop fusion | bytes 3732480 | tf_op jit(solution)/shard_map/broadcast_in_dim | solution.py:772

commit v3 on v2

--- a/solution.py
+++ b/solution.py
@@ -39,9 +39,9 @@
 ):
     small, (
     S,
-    C, inverse, iidx, iwgt, ridx, rwgt, mean, wr, wx, wy, sx0, sy0, rx0, ry0, sx, sy, rx, ry, rst, fb, xstrip, ystrip,
+    C, inverse, iidx, iwgt, ridx, rwgt, saved, racc, wr, wx, wy, sx0, sy0, rx0, ry0, sx, sy, rx, ry, rst, fb, xstrip, ystrip,
     load_sem, halo_send, halo_recv, strip_send, strip_recv, fb_send, fb_recv,
-    q0, q1, q2, xpack, ypack, q_send, q_recv,
+    q0, xpack, ypack, q_send, q_recv,
     ) = rest[:5], rest[5:]
     g, a, b = lax.axis_index("grp"), lax.axis_index("gx"), lax.axis_index("gy")
     nx, ny, lev = state.shape[2], state.shape[3], state.shape[4]
@@ -86,41 +86,21 @@
 
     def route(at_a, at_b):
         to_a, to_b = fx + at_a // 3, fy + at_b // 3
-        far = (at_a != to_a) & (at_b != to_b)
-        direct = (at_a == to_a) & (at_b == to_b)
-        over = jnp.logical_not(direct)
-        along_a = over & (at_a % 3 == 1) & far
-        along_b = over & (at_a % 3 == 0) & far
-        last = over & jnp.logical_not(along_a | along_b)
-        return to_a, to_b, direct, over, along_a, along_b, last
-
-    to_a, to_b, direct, over, along_a, along_b, last = route(a, b)
+        return to_a, to_b, (at_a % 3 == 0) & (at_a != to_a)
+
+    to_a, to_b, via = route(a, b)
     parent, nest = g == 0, g == 1
-    mid_a = 3 * (a - fx) + 1
-    comes = (a >= fx) & (mid_a < cx)
-    relay1 = parent & comes & route(mid_a, b)[4]
-    relay2 = []
+    greet(nest & via, (0, a, to_b))
+    relayed = []
     for j in range(3):
-        side_b = 3 * (b - fy) + j
-        relay2.append((parent & (b >= fy) & (side_b < cy) & route(a, side_b)[5], side_b))
-    greet(nest & over, (0, a, b))
-    greet(parent & over, (1, a, b))
-    greet(parent & along_a, (0, to_a, b))
-    greet(relay1, (0, mid_a, b))
-    greet(parent & along_b, (0, a, to_b))
-    for on, side_b in relay2:
-        greet(on, (0, a, side_b))
-        greet(on, (0, to_a, b))
-    greet(parent & last, (0, to_a, to_b))
-    greet(relay1, (0, a, to_b))
+        from_b = 3 * (b - fy) + j
+        on = parent & (b >= fy) & (from_b < cy) & via
+        relayed.append(on)
+        greet(on, (1, a, from_b))
+    greet(relayed[0], (0, to_a, b))
     for i in range(3):
-        for j in range(3):
-            from_a, from_b = 3 * (a - fx) + i, 3 * (b - fy) + j
-            on = parent & (a >= fx) & (b >= fy) & (from_a < cx) & (from_b < cy)
-            f_a, f_b, f_last = route(from_a, from_b)[4:]
-            greet(on & f_a, (0, a, from_b))
-            greet(on & f_b, (0, from_a, b))
-            greet(on & f_last, (0, from_a, from_b))
+        from_a = 3 * (a - fx) + i
+        greet(parent & (a >= fx) & (b >= fy) & (from_a < cx) & route(from_a, 0)[2], (0, from_a, b))
 
     loads = [
         pltpu.make_async_copy(
@@ -180,7 +160,7 @@
             def _():
                 halo_copy(k, d).wait_send()
 
-    def exchange(k):
+    def send_edges(k):
         cols = slice(YB, YB + ny)
         rows = slice(XB, XB + nx)
         last_x, last_y = XB + nx, YB + ny
@@ -208,17 +188,12 @@
             @pl.when(dirs[d][0])
             def _():
                 halo_copy(k, d).start()
-        if k == 0:
-            @pl.when(g == 1)
-            def _():
-                with jax.named_scope("restrict_weights"):
-                    restrict_weights()
-        if k == 1:
-            @pl.when((g == 1) & ((a == 0) | (a == cx - 1) | (b == 0) | (b == cy - 1)))
-            def _():
-                with jax.named_scope("boundary_weights"):
-                    boundary_weights()
-        for d in range(4):
+
+    def receive(k, which):
+        cols = slice(YB, YB + ny)
+        rows = slice(XB, XB + nx)
+        last_x, last_y = XB + nx, YB + ny
+        for d in which:
             @pl.when(dirs[d][1])
             def _():
                 halo_copy(k, d).wait_recv()
@@ -239,61 +214,79 @@
                         S[2, rows, at : at + 1, :] = got[:, 2:3]
                         C[1 : 1 + nx, at : at + 1, :] = got[:, 3:4]
 
-    def add_mean(k, c, x, value):
-        mean[c, x] = value if k == 0 else mean[c, x] + value
-
-    def winds(k):
-        def u_row(r, _):
-            slope = 0.5 * (S[0, r + 1, YB : YB + ny, :] - S[0, r - 1, YB : YB + ny, :])
-            S[1, r, YB : YB + ny, :] = S[1, r, YB : YB + ny, :] - C[r - 1, YB : YB + ny, :] * slope
+    cols = slice(YB, YB + ny)
+
+    def u_row(r):
+        slope = 0.5 * (S[0, r + 1, cols, :] - S[0, r - 1, cols, :])
+        return S[1, r, cols, :] - C[r - 1, cols, :] * slope
+
+    def v_row(r):
+        mid = slice(YB + 1, YB + ny - 1)
+        slope = 0.5 * (S[0, r, YB + 2 : YB + ny, :] - S[0, r, YB : YB + ny - 2, :])
+        return S[2, r, mid, :] - C[r - 1, mid, :] * slope
+
+    def inner_winds():
+        group = 4
+
+        def some(us, vs):
+            new = [(1, r, cols, u_row(r)) for r in us]
+            new += [(2, r, slice(YB + 1, YB + ny - 1), v_row(r)) for r in vs]
+            for c, r, at, value in new:
+                S[c, r, at, :] = value
+
+        def rows(i, _):
+            some(*[[XB + 2 + i * group + j for j in range(group)]] * 2)
             return 0
 
-        u_row(XB - 1, 0)
-        u_row(XB + nx, 0)
-
-        cols, wide = slice(YB, YB + ny), slice(YB - 1, YB + ny + 1)
-        group = 4
+        first, last = XB, XB + nx - 1
+        some((first + 1, last - 1), (first, first + 1, last - 1, last))
+        lax.fori_loop(0, (nx - 4) // group, rows, 0)
+
+    def edge_winds_x():
+        new = [(r, u_row(r)) for r in (XB - 1, XB, XB + nx - 1, XB + nx)]
+        for r, value in new:
+            S[1, r, cols, :] = value
+
+    def edge_winds_y():
+        rows = slice(XB, XB + nx)
+        for y in (YB - 1, YB + ny - 1):
+            slope = 0.5 * (S[0, rows, y + 1 : y + 3, :] - S[0, rows, y - 1 : y + 1, :])
+            S[2, rows, y : y + 2, :] = S[2, rows, y : y + 2, :] - C[1 : 1 + nx, y : y + 2, :] * slope
+
+    def forced(r, y, width):
+        at = slice(y, y + width)
+        div = 0.5 * (S[1, r + 1, at, :] - S[1, r - 1, at, :]) + 0.5 * (
+            S[2, r, y + 1 : y + width + 1, :] - S[2, r, y - 1 : y + width - 1, :]
+        )
+        return S[0, r, at, :] - C[r - 1, at, :] * div
+
+    def solved(parts):
+        return dot3(jnp.concatenate(parts, axis=0), m_high, m_low)
+
+    def inner_pressure():
+        group = 8
 
         def rows(i, _):
-            new = []
+            first = XB + 2 + i * group
+            new = solved([forced(first + j, YB, ny) for j in range(group)])
             for j in range(group):
-                x = i * group + j
-                r = x + XB
-                slope = 0.5 * (S[0, r + 1, cols, :] - S[0, r - 1, cols, :])
-                u = S[1, r, cols, :] - C[x + 1, cols, :] * slope
-                slope = 0.5 * (S[0, r, YB : YB + ny + 2, :] - S[0, r, YB - 2 : YB + ny, :])
-                v = S[2, r, wide, :] - C[x + 1, wide, :] * slope
-                new.append((x, u, v))
-            for x, u, v in new:
-                S[1, x + XB, cols, :] = u
-                S[2, x + XB, wide, :] = v
-                add_mean(k, 1, x, u)
-                add_mean(k, 2, x, v[1 : ny + 1])
+                S[0, first + j, YB + 2 : YB + ny - 2, :] = new[j * ny + 2 : (j + 1) * ny - 2]
             return 0
 
-        lax.fori_loop(0, nx // group, rows, 0)
-
-    def press(k):
-        group = 12
-
-        def rows(i, _):
-            parts = []
-            for j in range(group):
-                x = i * group + j
-                r = x + XB
-                div = 0.5 * (S[1, r + 1, YB : YB + ny, :] - S[1, r - 1, YB : YB + ny, :]) + 0.5 * (
-                    S[2, r, YB + 1 : YB + ny + 1, :] - S[2, r, YB - 1 : YB + ny - 1, :]
-                )
-                parts.append(S[0, r, YB : YB + ny, :] - C[x + 1, YB : YB + ny, :] * div)
-            solved = dot3(jnp.concatenate(parts, axis=0), m_high, m_low)
-            for j in range(group):
-                x = i * group + j
-                new = solved[j * ny : (j + 1) * ny]
-                S[0, x + XB, YB : YB + ny, :] = new
-                add_mean(k, 0, x, new)
-            return 0
-
-        lax.fori_loop(0, nx // group, rows, 0)
+        lax.fori_loop(0, (nx - 4) // group, rows, 0)
+
+    def edge_pressure():
+        rows = (XB, XB + 1, XB + nx - 2, XB + nx - 1)
+        parts = [forced(r, YB, ny) for r in rows]
+        sides = [(r, y) for y in (YB, YB + ny - 8) for r in range(XB + 2, XB + nx - 2)]
+        parts += [forced(r, y, 8) for r, y in sides]
+        new = solved(parts)
+        for n, r in enumerate(rows):
+            S[0, r, cols, :] = new[n * ny : (n + 1) * ny]
+        base = len(rows) * ny
+        for n, (r, y) in enumerate(sides):
+            skip = 0 if y == YB else 6
+            S[0, r, y + skip : y + skip + 2, :] = new[base + 8 * n + skip : base + 8 * n + skip + 2]
 
     def hop(src, dst, device, send, recv):
         return pltpu.make_async_remote_copy(
@@ -301,81 +294,71 @@
             device_id=device, device_id_type=MESH,
         )
 
-    def home(src, c, i, j, device, send):
+    chunks = ((1, slice(3, 3 * quarter)), (1, slice(0, 3)), (2, slice(0, 3 * quarter)))
+
+    def home(src, c, part, i, j, device, send):
         n = 3 * i + j
-        return hop(src, fb.at[n, c], device, send, fb_recv.at[n, min(c, 1)])
-
-    def fb_copies(c):
-        mine, sem = rst.at[c], fb_send.at[min(c, 1)]
-        straight = home(mine, c, a % 3, b % 3, (0, to_a, to_b), sem)
-        if c == 0:
-            return ((nest, straight),)
-        return (
-            (direct, straight),
-            (over, hop(mine, q0.at[c - 1], (0, a, b), sem, q_recv.at[0, c - 1])),
-        )
-
-    def fb_start(c):
-        for on, copy in fb_copies(c):
-            @pl.when(on)
-            def _():
-                copy.start()
-
-    def relays(c):
-        n = c - 1
-        sem0 = q_send.at[0]
-        yield parent & over, q0, 0, (
-            (along_a, hop(q0.at[n], q1.at[n], (0, to_a, b), sem0, q_recv.at[1, n])),
-            (along_b, hop(q0.at[n], q2.at[b % 3, n], (0, a, to_b), sem0,
-                          q_recv.at[2 + b % 3, n])),
-            (last, home(q0.at[n], c, a % 3, b % 3, (0, to_a, to_b), sem0)),
-        )
-        yield relay1, q1, 1, (
-            (relay1, home(q1.at[n], c, 1, b % 3, (0, a, to_b), q_send.at[1])),
-        )
-        for j, (on, side_b) in enumerate(relay2):
-            yield on, q2.at[j], 2 + j, (
-                (on, home(q2.at[j, n], c, 0, j, (0, to_a, b), q_send.at[2 + j])),
-            )
+        return hop(src, fb.at[n, c, part], device, send, fb_recv.at[n, min(c, 1)])
+
+    def pressure_home():
+        whole = slice(0, 3 * quarter)
+        return home(rst.at[0], 0, whole, a % 3, b % 3, (0, to_a, to_b), fb_send.at[0])
+
+    def fb_start(n):
+        c, part = chunks[n]
+        mine, sem = rst.at[c, part], fb_send.at[1]
+
+        @pl.when(jnp.logical_not(via))
+        def _():
+            home(mine, c, part, a % 3, b % 3, (0, to_a, to_b), sem).start()
+
+        @pl.when(via)
+        def _():
+            hop(mine, q0.at[b % 3, c - 1, part], (0, a, to_b), sem, q_recv.at[b % 3, n]).start()
 
     def pass_on():
-        for stages in zip(relays(1), relays(2)):
-            for n, (here, buffer, stage, onward) in enumerate(stages):
-                @pl.when(here)
+        for n, (c, part) in enumerate(chunks):
+            for j in range(3):
+                @pl.when(relayed[j])
                 def _():
-                    piece = buffer.at[n]
-                    hop(piece, piece, (g, a, b), q_send.at[stage], q_recv.at[stage, n]).wait_recv()
-                    for on, copy in onward:
-                        @pl.when(on)
-                        def _():
-                            copy.start()
+                    piece = q0.at[j, c - 1, part]
+                    hop(piece, piece, (g, a, b), q_send.at[j], q_recv.at[j, n]).wait_recv()
+                    home(piece, c, part, 0, j, (0, to_a, b), q_send.at[j]).start()
 
     def passed_on():
-        for here, buffer, stage, _ in relays(1):
-            @pl.when(here)
-            def _():
-                hop(buffer, buffer, (g, a, b), q_send.at[stage], q_recv.at[0, 0]).wait_send()
-
-    def restrict(comps):
-        def mixed_row(c, u):
-            total = None
-            for t in range(9):
-                part = wr[u, t] * mean[c, 3 * u + t // 3, pl.ds(t % 3, ty, stride=3), :]
-                total = part if total is None else total + part
-            return total
-
-        def rows(i, _):
-            new = []
-            spare = jnp.zeros((ty, 128 - lev - slot), F32)
-            for c in comps:
-                guest = mixed_row(c, 3 * quarter + i)
-                for m in range(3):
-                    new.append((c, 3 * i + m, mixed_row(c, 3 * i + m), guest[:, m * slot : (m + 1) * slot]))
-            for c, u, own, part in new:
-                rst[c, u] = jnp.concatenate([own, part, spare], axis=1)
+        for j in range(3):
+            @pl.when(relayed[j])
+            def _():
+                hop(q0.at[j], q0.at[j], (g, a, b), q_send.at[j], q_recv.at[0, 0]).wait_send()
+
+    def rows_of(i):
+        if i == 0:
+            return 0, tx - 1, 1, 2
+        return tuple(4 * i - 1 + m for m in range(4))
+
+    def mixed_row(c, u):
+        total = None
+        for t in range(9):
+            part = wr[u, t] * S[c, XB + 3 * u + t // 3, pl.ds(YB + t % 3, ty, stride=3), :]
+            total = part if total is None else total + part
+        return total
+
+    def gather_mean(k):
+        def rows(u, _):
+            new = [mixed_row(c, u) for c in range(3)]
+            for c in range(3):
+                racc[c, u] = new[c] if k == 0 else racc[c, u] + new[c]
             return 0
 
-        lax.fori_loop(0, quarter, rows, 0)
+        lax.fori_loop(0, tx, rows, 0)
+
+    def restrict(c, groups):
+        spare = jnp.zeros((ty, 128 - lev - slot), F32)
+        for i in groups:
+            own = [racc[c, u] + mixed_row(c, u) for u in rows_of(i)]
+            for m in range(3):
+                part = own[3][:, m * slot : (m + 1) * slot]
+                rst[c, 3 * i + m] = jnp.concatenate([own[m], part, spare], axis=1)
 
     def restrict_weights():
         terms = range(ridx.shape[0])
@@ -561,28 +544,68 @@
         )
         for c in range(3):
             bound = mixed(wx[...], xstrip[c].reshape(3 * (ty + 16), lev)).reshape(shape)
-            now = mean[c, 0:BAND]
+            now = saved[c]
             S[c, XB + first : XB + first + BAND, YB : YB + ny, :] = now + relax * (bound - now)
 
     for k in range(SUBS):
-        with jax.named_scope(f"exchange{k}"):
-            exchange(k)
-        with jax.named_scope(f"winds{k}"):
-            winds(k)
-        if k == SUBS - 1:
+        with jax.named_scope(f"send{k}"):
+            send_edges(k)
+
+        @pl.when(g == 1)
+        def _():
+            if k == 0:
+                with jax.named_scope("restrict_weights"):
+                    restrict_weights()
+            else:
+                with jax.named_scope(f"mean{k}"):
+                    gather_mean(k - 1)
+
+        last = k == SUBS - 1
+        with jax.named_scope(f"inner_winds{k}"):
+            inner_winds()
+        if last:
             @pl.when(g == 1)
             def _():
-                with jax.named_scope("restrict_winds"):
-                    restrict((1, 2))
+                with jax.named_scope("restrict_u"):
+                    restrict(1, range(1, quarter))
+                fb_start(0)
+
+        with jax.named_scope(f"inner_pressure{k}"):
+            inner_pressure()
+        if k == 1:
+            @pl.when((g == 1) & ((a == 0) | (a == cx - 1) | (b == 0) | (b == cy - 1)))
+            def _():
+                with jax.named_scope("boundary_weights"):
+                    boundary_weights()
+        with jax.named_scope(f"receive_y{k}"):
+            receive(k, (2, 3))
+        edge_winds_y()
+        if last:
+            @pl.when(g == 1)
+            def _():
+                with jax.named_scope("restrict_v"):
+                    restrict(2, range(quarter))
+                fb_start(2)
+
+            @pl.when(g == 0)
+            def _():
+                strip_pack((2,))
+                strip_start(slice(2, 3))
+        with jax.named_scope(f"receive_x{k}"):
+            receive(k, (0, 1))
+        edge_winds_x()
+        if last:
+            @pl.when(g == 1)
+            def _():
+                restrict(1, (0,))
                 fb_start(1)
-                fb_start(2)
 
             @pl.when(g == 0)
             def _():
-                strip_pack((1, 2))
-                strip_start(slice(1, 3))
-        with jax.named_scope(f"press{k}"):
-            press(k)
+                strip_pack((1,))
+                strip_start(slice(1, 2))
+        with jax.named_scope(f"edge_pressure{k}"):
+            edge_pressure()
 
     def take(i, j, comps):
         first, count = comps[0], len(comps)
@@ -594,24 +617,20 @@
                 device_id_type=MESH,
             ).wait_recv()
         for c in comps:
-            got = fb[3 * i + j, c]
-            parts = got.reshape(quarter, 3, ty, 128)[:, :, :, lev : lev + slot]
-            guest = jnp.concatenate([parts[:, m] for m in range(3)], axis=2)
-
-            def blend(u, count, value):
-                first = XB + i * tx + u
-                at = (c, slice(first, first + count), slice(YB + j * ty, YB + (j + 1) * ty), slice(None))
-                now = S[at]
-                S[at] = now + FEEDBACK * (value - now)
-
-            blend(0, 3 * quarter, got[:, :, :lev])
-            blend(3 * quarter, quarter, guest)
+            for n in range(quarter):
+                got = fb[3 * i + j, c, 3 * n : 3 * n + 3]
+                rows = [got[m, :, :lev] for m in range(3)]
+                rows.append(jnp.concatenate([got[m, :, lev : lev + slot] for m in range(3)], axis=1))
+                for u, value in zip(rows_of(n), rows):
+                    at = (c, XB + i * tx + u, slice(YB + j * ty, YB + (j + 1) * ty), slice(None))
+                    now = S[at]
+                    S[at] = now + FEEDBACK * (value - now)
 
     @pl.when(g == 1)
     def _():
         with jax.named_scope("restrict_pressure"):
-            restrict((0,))
-        fb_start(0)
+            restrict(0, range(quarter))
+        pressure_home().start()
         halo_sent(SUBS - 1)
         x_low, x_high = a == 0, a == cx - 1
         y_low, y_high = b == 0, b == cy - 1
@@ -619,12 +638,12 @@
         @pl.when(x_low)
         def _():
             for c in range(3):
-                mean[c, 0:BAND] = S[c, XB : XB + BAND, YB : YB + ny, :]
+                saved[c] = S[c, XB : XB + BAND, YB : YB + ny, :]
 
         @pl.when(x_high)
         def _():
             for c in range(3):
-                mean[c, 0:BAND] = S[c, XB + nx - BAND : XB + nx, YB : YB + ny, :]
+                saved[c] = S[c, XB + nx - BAND : XB + nx, YB : YB + ny, :]
 
         @pl.when(x_low | x_high)
         def _():
@@ -693,9 +712,10 @@
         halo_sent(SUBS - 1)
         passed_on()
         winds_of, pressure_of = (1, 2), (0,)
-        order = [((2, j), winds_of) for j in (2, 1, 0)] + [((2, j), pressure_of) for j in (2, 1, 0)]
-        order += [((1, 2), winds_of)] + [((i, j), pressure_of) for i in (1, 0) for j in (2, 1, 0)]
-        order += [(at, winds_of) for at in ((1, 1), (1, 0), (0, 2), (0, 1), (0, 0))]
+        near = [(i, j) for i in (2, 1) for j in (2, 1, 0)]
+        far = [(0, j) for j in (2, 1, 0)]
+        order = [(at, winds_of) for at in near] + [(at, pressure_of) for at in near + far]
+        order += [(at, winds_of) for at in far]
         for (i, j), comps in order:
             there = (a >= fx) & (b >= fy) & (3 * (a - fx) + i < cx) & (3 * (b - fy) + j < cy)
 
@@ -729,7 +749,8 @@
             vmem(nx, 4, ny),
             pltpu.VMEM((9, tx, ty), jnp.int32),
             vmem(9, tx, ty),
-            vmem(3, nx, ny, lev),
+            vmem(3, BAND, ny, lev),
+            vmem(3, tx, ty, lev),
             vmem(tx, 9, ty, lev),
             vmem(BAND * ny, 3 * (ty + 16)),
             vmem(nx * 8, 4 * (tx + 2)),
@@ -752,13 +773,11 @@
             dma((2, 3)),
             dma((2,)),
             dma((9, 2)),
-            vmem(2, *packed),
-            vmem(2, *packed),
             vmem(3, 2, *packed),
             vmem(3, 3, ny, lev),
             vmem(3, nx, 4, lev),
-            dma((5,)),
-            dma((5, 2)),
+            dma((3,)),
+            dma((3, 3)),
         ],
         compiler_params=pltpu.CompilerParams(
             has_side_effects=True, collective_id=0, vmem_limit_bytes=67043328 - 4 * (3 * (nx + 4) * (ny + 16) * 128) - 2**14

time: 40.8 us -> 32.4 us (0.79)
  Pallas kernels: 39 us -> 30.2 us
    pallas_call x1, Pallas kernels: 39 us -> 30.2 us  [per_device(): pl.pallas_call(functools.partial(kernel, cx, cy), out_shape=vmem(3, nx +...]
where the time goes in v3:
time: 32.4 us; the launch traced here: 31.9 us
  Pallas kernels  30.2 us (93%)
  local copies, waits for them, and re-layouts  1.73 us (5%)
    pallas_call x1, Pallas kernels, per_device(): pl.pallas_call(functools.partial(kernel, cx, cy), out_shape=vmem(3, nx +...  30.2 us
    broadcast_in_dim x1, local copies, waits for them, and re-layouts, per_device(): return padded[None, :, XB:XB + nx, YB:YB + ny, :]  1.73 us

profile of v3, /device:TPU:20, one launch (start us, length us, event | category | flops | bytes accessed | tf_op | source)
XLA Modules:
  0.0 31.9 jit_solution(11782183228488527408)
XLA Ops:
  0.0 30.2 %nest_step.1 = f32[3,40,64,90]{3,2,1,0:T(8,128)S(1)} custom-call(f32[1,3,36,48,90]{4,3,2,1,0:T(8,128)} %state.1, f32[1,36,48,90]{3,2,1,0:T(8,128)} %courant.1, f32[90,1,90]{2,1,0:T(1,128)} %bitcast.11, s32[36,4,48]{2,1,0:T(4,128)} %bitcast.7, f32[36,4,48]{2,1,0:T(4,128)} %bitcast.8, s32[9,12,16]{2,1,0:T(8,128)} %bitcast.9, f32[9,12,16]{2,1,0:T(8,128)} %bitcast.10), custom_call_target="tpu_custom_call" | custom-call | tf_op jit(solution)/shard_map/nest_step/pallas_call | solution.py:740
  30.2 1.7 %slice_bitcast_fusion = f32[1,3,36,48,90]{4,3,2,1,0:T(8,128)} fusion(f32[3,40,64,90]{3,2,1,0:T(8,128)S(1)} %nest_step.1), kind=kLoop, calls=%fused_computation | loop fusion | bytes 3732480 | tf_op jit(solution)/shard_map/broadcast_in_dim | solution.py:791

commit v4 on v3

--- a/solution.py
+++ b/solution.py
@@ -39,9 +39,9 @@
 ):
     small, (
     S,
-    C, inverse, iidx, iwgt, ridx, rwgt, saved, racc, wr, wx, wy, sx0, sy0, rx0, ry0, sx, sy, rx, ry, rst, fb, xstrip, ystrip,
+    C, inverse, iidx, iwgt, ridx, rwgt, saved, racc, wr, wx, wy, sx0, sy0, rx0, ry0, sx, sy, rx, ry, rst, fb, xstrip, xouter, ystrip,
     load_sem, halo_send, halo_recv, strip_send, strip_recv, fb_send, fb_recv,
-    q0, xpack, ypack, q_send, q_recv,
+    q0, xpack, outer, ypack, q_send, q_recv, outer_send,
     ) = rest[:5], rest[5:]
     g, a, b = lax.axis_index("grp"), lax.axis_index("gx"), lax.axis_index("gy")
     nx, ny, lev = state.shape[2], state.shape[3], state.shape[4]
@@ -59,10 +59,6 @@
         def _():
             pl.semaphore_signal(barrier, inc=1, device_id=device, device_id_type=MESH)
 
-    greet(a > 0, (g, a - 1, b))
-    greet(a < cx - 1, (g, a + 1, b))
-    greet(b > 0, (g, a, b - 1))
-    greet(b < cy - 1, (g, a, b + 1))
     for i in range(-1, 4):
         for j in range(-1, 4):
             child_a, child_b = 3 * (a - fx) + i, 3 * (b - fy) + j
@@ -83,24 +79,6 @@
     for on_a, parent_a in parents(a, fx, cx):
         for on_b, parent_b in parents(b, fy, cy):
             greet((g == 1) & on_a & on_b, (0, parent_a, parent_b))
-
-    def route(at_a, at_b):
-        to_a, to_b = fx + at_a // 3, fy + at_b // 3
-        return to_a, to_b, (at_a % 3 == 0) & (at_a != to_a)
-
-    to_a, to_b, via = route(a, b)
-    parent, nest = g == 0, g == 1
-    greet(nest & via, (0, a, to_b))
-    relayed = []
-    for j in range(3):
-        from_b = 3 * (b - fy) + j
-        on = parent & (b >= fy) & (from_b < cy) & via
-        relayed.append(on)
-        greet(on, (1, a, from_b))
-    greet(relayed[0], (0, to_a, b))
-    for i in range(3):
-        from_a = 3 * (a - fx) + i
-        greet(parent & (a >= fx) & (b >= fy) & (from_a < cx) & route(from_a, 0)[2], (0, from_a, b))
 
     loads = [
         pltpu.make_async_copy(
@@ -114,6 +92,41 @@
         loads.append(pltpu.make_async_copy(src, dst, load_sem.at[2 + n]))
     for copy in loads:
         copy.start()
+
+    def relay_of(at_a):
+        to_a = fx + at_a // 3
+        back = (at_a % 3 == 0) & (at_a != to_a)
+        on = (at_a % 3 == 2) & (to_a + 1 < cx)
+        return to_a, back, on
+
+    to_a, back, on_next = relay_of(a)
+    to_b = fy + b // 3
+    parent, nest = g == 0, g == 1
+    via = back | on_next
+    relay_a = jnp.where(back, a, to_a + 1)
+    greet(nest & via, (0, relay_a, to_b))
+    relayed = []
+    next_a = 3 * (a - 1 - fx) + 2
+    for from_a, lane, i, here in (
+        (a, 0, 0, back), (next_a, 1, 2, (a - 1 >= fx) & (next_a < cx)),
+    ):
+        for j in range(3):
+            from_b = 3 * (b - fy) + j
+            on = parent & here & (b >= fy) & (from_b < cy)
+            relayed.append((on, 3 * lane + j, i, j, fx + from_a // 3))
+            greet(on, (1, from_a, from_b))
+        greet(relayed[-3][0], (0, fx + from_a // 3, b))
+    for i in range(3):
+        from_a = 3 * (a - fx) + i
+        on = parent & (a >= fx) & (b >= fy) & (from_a < cx)
+        _, from_back, from_next = relay_of(from_a)
+        greet(on & from_back, (0, from_a, b))
+        greet(on & from_next, (0, a + 1, b))
+
+    greet(a > 0, (g, a - 1, b))
+    greet(a < cx - 1, (g, a + 1, b))
+    greet(b > 0, (g, a, b - 1))
+    greet(b < cy - 1, (g, a, b + 1))
     zrow = jnp.zeros((2, ny, lev), F32)
     S[0, 0:2, YB : YB + ny, :] = zrow
     S[0, XB + nx : XB + nx + 2, YB : YB + ny, :] = zrow
@@ -121,6 +134,7 @@
     S[1, XB + nx : XB + nx + 2, YB : YB + ny, :] = zrow
     C[0:1, YB : YB + ny, :] = zrow[0:1]
     C[nx + 1 : nx + 2, YB : YB + ny, :] = zrow[0:1]
+    outer[...] = jnp.zeros((2, 3, 3, 4, lev), F32)
     zcol = jnp.zeros((nx, 8, lev), F32)
     for c in (0, 2):
         S[c, XB : XB + nx, 0:YB, :] = zcol
@@ -160,10 +174,10 @@
             def _():
                 halo_copy(k, d).wait_send()
 
-    def send_edges(k):
-        cols = slice(YB, YB + ny)
+    def send_edges(k, which):
         rows = slice(XB, XB + nx)
         last_x, last_y = XB + nx, YB + ny
+        cols = slice(YB, last_y)
         if k == 0:
             sx0[0, 0:2] = S[0, XB : XB + 2, cols, :]
             sx0[0, 2:3] = S[1, XB : XB + 1, cols, :]
@@ -177,16 +191,17 @@
             sy0[1, :, 0:2] = S[0, rows, last_y - 2 : last_y, :]
             sy0[1, :, 2:3] = S[2, rows, last_y - 1 : last_y, :]
             sy0[1, :, 3:4] = C[1 : 1 + nx, last_y - 1 : last_y, :]
-        else:
+        elif 0 in which:
             sx[k - 1, 0] = S[0, XB : XB + 2, cols, :]
             sx[k - 1, 1] = S[0, last_x - 2 : last_x, cols, :]
+        else:
             sy[k - 1, 0] = S[0, rows, YB : YB + 2, :]
             sy[k - 1, 1] = S[0, rows, last_y - 2 : last_y, :]
-        if k > 0:
-            halo_sent(k - 1)
-        for d in range(4):
+        for d in which:
             @pl.when(dirs[d][0])
             def _():
+                if k > 0:
+                    halo_copy(k - 1, d).wait_send()
                 halo_copy(k, d).start()
 
     def receive(k, which):
@@ -275,18 +290,18 @@
 
         lax.fori_loop(0, (nx - 4) // group, rows, 0)
 
-    def edge_pressure():
+    def edge_rows():
         rows = (XB, XB + 1, XB + nx - 2, XB + nx - 1)
-        parts = [forced(r, YB, ny) for r in rows]
-        sides = [(r, y) for y in (YB, YB + ny - 8) for r in range(XB + 2, XB + nx - 2)]
-        parts += [forced(r, y, 8) for r, y in sides]
-        new = solved(parts)
+        new = solved([forced(r, YB, ny) for r in rows])
         for n, r in enumerate(rows):
             S[0, r, cols, :] = new[n * ny : (n + 1) * ny]
-        base = len(rows) * ny
+
+    def edge_columns():
+        sides = [(r, y) for y in (YB, YB + ny - 8) for r in range(XB + 2, XB + nx - 2)]
+        new = solved([forced(r, y, 8) for r, y in sides])
         for n, (r, y) in enumerate(sides):
             skip = 0 if y == YB else 6
-            S[0, r, y + skip : y + skip + 2, :] = new[base + 8 * n + skip : base + 8 * n + skip + 2]
+            S[0, r, y + skip : y + skip + 2, :] = new[8 * n + skip : 8 * n + skip + 2]
 
     def hop(src, dst, device, send, recv):
         return pltpu.make_async_remote_copy(
@@ -294,7 +309,7 @@
             device_id=device, device_id_type=MESH,
         )
 
-    chunks = ((1, slice(3, 3 * quarter)), (1, slice(0, 3)), (2, slice(0, 3 * quarter)))
+    chunks = ((1, slice(3, 3 * quarter)), (2, slice(0, 3 * quarter)), (1, slice(0, 3)))
 
     def home(src, c, part, i, j, device, send):
         n = 3 * i + j
@@ -307,29 +322,33 @@
     def fb_start(n):
         c, part = chunks[n]
         mine, sem = rst.at[c, part], fb_send.at[1]
-
-        @pl.when(jnp.logical_not(via))
+        around = via if n < 2 else back
+
+        @pl.when(jnp.logical_not(around))
         def _():
             home(mine, c, part, a % 3, b % 3, (0, to_a, to_b), sem).start()
 
-        @pl.when(via)
-        def _():
-            hop(mine, q0.at[b % 3, c - 1, part], (0, a, to_b), sem, q_recv.at[b % 3, n]).start()
+        @pl.when(around)
+        def _():
+            at = jnp.where(back, 0, 3) + b % 3
+            hop(mine, q0.at[at, c - 1, part], (0, relay_a, to_b), sem, q_recv.at[at, n]).start()
 
     def pass_on():
         for n, (c, part) in enumerate(chunks):
-            for j in range(3):
-                @pl.when(relayed[j])
+            for on, at, i, j, home_a in relayed[: 6 if n < 2 else 3]:
+                @pl.when(on)
                 def _():
-                    piece = q0.at[j, c - 1, part]
-                    hop(piece, piece, (g, a, b), q_send.at[j], q_recv.at[j, n]).wait_recv()
-                    home(piece, c, part, 0, j, (0, to_a, b), q_send.at[j]).start()
+                    piece = q0.at[at, c - 1, part]
+                    hop(piece, piece, (g, a, b), q_send.at[at], q_recv.at[at, n]).wait_recv()
+                    home(piece, c, part, i, j, (0, home_a, b), q_send.at[at]).start()
 
     def passed_on():
-        for j in range(3):
-            @pl.when(relayed[j])
-            def _():
-                hop(q0.at[j], q0.at[j], (g, a, b), q_send.at[j], q_recv.at[0, 0]).wait_send()
+        for on, at, _, _, _ in relayed:
+            @pl.when(on)
+            def _():
+                sent = [q0.at[at]] if at < 3 else [q0.at[at, 0, chunks[0][1]], q0.at[at, 1]]
+                for piece in sent:
+                    hop(piece, piece, (g, a, b), q_send.at[at], q_recv.at[0, 0]).wait_send()
 
     def rows_of(i):
         if i == 0:
@@ -396,10 +415,12 @@
                 wy[8 * x : 8 * x + 8] = spread(cells, parts, x, 4 * (tx + 2))
 
         def x_weights(first, strip0):
-            wide = ty + 16
-            cells = (source_x - (a * tx + strip0)) * wide + source_y - (b * ty - 8)
+            row, column = source_x - (a * tx + strip0), source_y - b * ty
+            cells = jnp.where(
+                column < 0, 3 * ty + row, jnp.where(column < ty, row * ty + column, 3 * ty + 4 + row)
+            )
             for i in range(BAND):
-                wx[ny * i : ny * i + ny] = spread(cells, share, first + i, 3 * wide)
+                wx[ny * i : ny * i + ny] = spread(cells, share, first + i, 3 * ty + 8)
 
         @pl.when(b == 0)
         def _():
@@ -423,8 +444,6 @@
             total = total + row
         return total
 
-    x_windows = {-1: (0, 8, 24), 0: (0, ty + 8, 8), 1: (ty - 8, 2 * ty + 8, 0),
-                 2: (2 * ty - 8, ny, 0), 3: (ny - 8, ny, 0)}
     y_windows = {-1: (0, 1, tx + 1), 0: (0, tx + 1, 1), 1: (tx - 1, 2 * tx + 1, 0),
                  2: (2 * tx - 1, nx, 0), 3: (nx - 1, nx, 0)}
     kinds = {-1: 1, 0: 0, 1: 0, 2: 0, 3: 2}
@@ -447,6 +466,9 @@
             def _():
                 for c in comps:
                     xpack[c] = S[c, x_at : x_at + 3, YB : YB + ny, :]
+                    for j in range(3):
+                        for side_y, y in ((1, j * ty), (0, j * ty + ty - 1)):
+                            outer[side_y, j, c, 0:3] = S[c, x_at : x_at + 3, YB + y, :]
 
             _, on, y_at = y_side(side)
 
@@ -458,15 +480,21 @@
     def strip_copies(comps):
         for side in range(2):
             edge, here, _ = x_side(side)
-            for j in range(-1, 4):
-                lo, hi, dst = x_windows[j]
+            for j in range(3):
                 child = 3 * (b - fy) + j
-                yield here & (child >= 0) & (child < cy), pltpu.make_async_remote_copy(
-                    src_ref=xpack.at[comps, :, pl.ds(lo, hi - lo), :],
-                    dst_ref=xstrip.at[comps, :, pl.ds(dst, hi - lo), :],
-                    send_sem=strip_send.at[0, j + 1], recv_sem=strip_recv.at[0, kinds[j]],
+                yield here & (child < cy), pltpu.make_async_remote_copy(
+                    src_ref=xpack.at[comps, :, pl.ds(j * ty, ty), :], dst_ref=xstrip.at[comps],
+                    send_sem=strip_send.at[0, j], recv_sem=strip_recv.at[0, 0],
                     device_id=(1, edge, child), device_id_type=MESH,
                 )
+                if comps.start > 0:
+                    continue
+                for side_y, beside in ((0, child + 1), (1, child - 1)):
+                    yield here & (child < cy) & (beside >= 0) & (beside < cy), pltpu.make_async_remote_copy(
+                        src_ref=outer.at[side_y, j], dst_ref=xouter.at[side_y],
+                        send_sem=outer_send.at[side_y, j], recv_sem=strip_recv.at[0, 1 + side_y],
+                        device_id=(1, edge, beside), device_id_type=MESH,
+                    )
             edge, here, _ = y_side(side)
             for i in range(-1, 4):
                 lo, hi, dst = y_windows[i]
@@ -490,29 +518,39 @@
             def _():
                 copy.wait_send()
 
-    def strip_wait(axis, kind, lo, hi, dst):
-        if axis == 0:
-            ref = xstrip.at[:, :, pl.ds(dst, hi - lo), :]
-        else:
-            ref = ystrip.at[:, pl.ds(dst, hi - lo), :, :]
+    def strip_wait(ref, kind):
         pltpu.make_async_remote_copy(
             src_ref=ref, dst_ref=ref, send_sem=strip_send.at[0, 0],
-            recv_sem=strip_recv.at[axis, kind], device_id=(g, a, b), device_id_type=MESH,
+            recv_sem=strip_recv.at[kind], device_id=(g, a, b), device_id_type=MESH,
         ).wait_recv()
 
-    def wait_strips(axis, place, count, windows):
+    def wait_y_strips():
+        def rows(kind, lo, hi, dst):
+            strip_wait(ystrip.at[:, pl.ds(dst, hi - lo), :, :], (1, kind))
+
         for i in range(3):
-            @pl.when(place % 3 == i)
-            def _():
-                strip_wait(axis, 0, *windows[i])
-
-        @pl.when((place % 3 == 2) & (place < count - 1))
-        def _():
-            strip_wait(axis, 1, *windows[-1])
-
-        @pl.when((place % 3 == 0) & (place > 0))
-        def _():
-            strip_wait(axis, 2, *windows[3])
+            @pl.when(a % 3 == i)
+            def _():
+                rows(0, *y_windows[i])
+
+        @pl.when((a % 3 == 2) & (a < cx - 1))
+        def _():
+            rows(1, *y_windows[-1])
+
+        @pl.when((a % 3 == 0) & (a > 0))
+        def _():
+            rows(2, *y_windows[3])
+
+    def wait_x_strips():
+        strip_wait(xstrip, (0, 0))
+
+        @pl.when(b > 0)
+        def _():
+            strip_wait(xouter.at[0], (0, 1))
+
+        @pl.when(b < cy - 1)
+        def _():
+            strip_wait(xouter.at[1], (0, 2))
 
     def relax_at(x, y):
         gx, gy = a * nx + x, b * ny + y
@@ -543,13 +581,16 @@
             first + lax.broadcasted_iota(jnp.int32, shape, 0), lax.broadcasted_iota(jnp.int32, shape, 1)
         )
         for c in range(3):
-            bound = mixed(wx[...], xstrip[c].reshape(3 * (ty + 16), lev)).reshape(shape)
+            source = jnp.concatenate(
+                [xstrip[c].reshape(3 * ty, lev), xouter[0, c], xouter[1, c]], axis=0
+            )
+            bound = mixed(wx[...], source).reshape(shape)
             now = saved[c]
             S[c, XB + first : XB + first + BAND, YB : YB + ny, :] = now + relax * (bound - now)
 
     for k in range(SUBS):
-        with jax.named_scope(f"send{k}"):
-            send_edges(k)
+        if k == 0:
+            send_edges(0, (0, 1, 2, 3))
 
         @pl.when(g == 1)
         def _():
@@ -585,7 +626,7 @@
             def _():
                 with jax.named_scope("restrict_v"):
                     restrict(2, range(quarter))
-                fb_start(2)
+                fb_start(1)
 
             @pl.when(g == 0)
             def _():
@@ -598,14 +639,20 @@
             @pl.when(g == 1)
             def _():
                 restrict(1, (0,))
-                fb_start(1)
+                fb_start(2)
 
             @pl.when(g == 0)
             def _():
                 strip_pack((1,))
                 strip_start(slice(1, 2))
-        with jax.named_scope(f"edge_pressure{k}"):
-            edge_pressure()
+        with jax.named_scope(f"edge_rows{k}"):
+            edge_rows()
+            if not last:
+                send_edges(k + 1, (0, 1))
+        with jax.named_scope(f"edge_columns{k}"):
+            edge_columns()
+            if not last:
+                send_edges(k + 1, (2, 3))
 
     def take(i, j, comps):
         first, count = comps[0], len(comps)
@@ -647,17 +694,13 @@
 
         @pl.when(x_low | x_high)
         def _():
-            xstrip_pad = jnp.zeros((3, 3, 8, lev), F32)
-
             @pl.when(y_low)
             def _():
-                xstrip[:, :, 0:8, :] = xstrip_pad
-
-            if (cy - 1) % 3 == 2:
-
-                @pl.when(y_high)
-                def _():
-                    xstrip[:, :, ty + 8 : ty + 16, :] = xstrip_pad
+                xouter[0] = jnp.zeros((3, 4, lev), F32)
+
+            @pl.when(y_high)
+            def _():
+                xouter[1] = jnp.zeros((3, 4, lev), F32)
 
         @pl.when(y_low | y_high)
         def _():
@@ -672,7 +715,7 @@
                     ystrip[:, tx + 1 : tx + 2] = jnp.zeros((3, 1, 4, lev), F32)
 
             with jax.named_scope("wait_y"):
-                wait_strips(1, a, cx, y_windows)
+                wait_y_strips()
 
         @pl.when(y_low)
         def _():
@@ -687,7 +730,7 @@
         @pl.when(x_low | x_high)
         def _():
             with jax.named_scope("wait_x"):
-                wait_strips(0, b, cy, x_windows)
+                wait_x_strips()
 
         @pl.when(x_low)
         def _():
@@ -712,10 +755,11 @@
         halo_sent(SUBS - 1)
         passed_on()
         winds_of, pressure_of = (1, 2), (0,)
-        near = [(i, j) for i in (2, 1) for j in (2, 1, 0)]
-        far = [(0, j) for j in (2, 1, 0)]
-        order = [(at, winds_of) for at in near] + [(at, pressure_of) for at in near + far]
-        order += [(at, winds_of) for at in far]
+        tiles = [[(i, j) for j in (2, 0, 1)] for i in range(3)]
+        order = [(at, winds_of) for at in tiles[1]] + [(at, pressure_of) for at in tiles[1]]
+        order += [(at, winds_of) for at in tiles[2]] + [(at, pressure_of) for at in tiles[0]]
+        order += [(at, pressure_of) for at in tiles[2][:2]] + [(at, winds_of) for at in tiles[0]]
+        order += [(at, pressure_of) for at in tiles[2][2:]]
         for (i, j), comps in order:
             there = (a >= fx) & (b >= fy) & (3 * (a - fx) + i < cx) & (3 * (b - fy) + j < cy)
 
@@ -752,7 +796,7 @@
             vmem(3, BAND, ny, lev),
             vmem(3, tx, ty, lev),
             vmem(tx, 9, ty, lev),
-            vmem(BAND * ny, 3 * (ty + 16)),
+            vmem(BAND * ny, 3 * ty + 8),
             vmem(nx * 8, 4 * (tx + 2)),
             vmem(2, 4, ny, lev),
             vmem(2, nx, 4, lev),
@@ -764,7 +808,8 @@
             vmem(SUBS - 1, 2, nx, 2, lev),
             vmem(3, *packed),
             vmem(9, 3, *packed),
-            vmem(3, 3, ty + 16, lev),
+            vmem(3, 3, ty, lev),
+            vmem(2, 3, 4, lev),
             vmem(3, tx + 2, 4, lev),
             dma((7,)),
             dma((4,)),
@@ -773,11 +818,13 @@
             dma((2, 3)),
             dma((2,)),
             dma((9, 2)),
-            vmem(3, 2, *packed),
+            vmem(6, 2, *packed),
             vmem(3, 3, ny, lev),
+            vmem(2, 3, 3, 4, lev),
             vmem(3, nx, 4, lev),
-            dma((3,)),
-            dma((3, 3)),
+            dma((6,)),
+            dma((6, 3)),
+            dma((2, 3)),
         ],
         compiler_params=pltpu.CompilerParams(
             has_side_effects=True, collective_id=0, vmem_limit_bytes=67043328 - 4 * (3 * (nx + 4) * (ny + 16) * 128) - 2**14

time: 32.4 us -> 30.5 us (0.941)
  Pallas kernels: 30.2 us -> 28.6 us
    pallas_call x1, Pallas kernels: 30.2 us -> 28.6 us  [per_device(): pl.pallas_call(functools.partial(kernel, cx, cy), out_shape=vmem(3, nx +...]
where the time goes in v4:
time: 30.5 us; the launch traced here: 30.4 us
  Pallas kernels  28.6 us (94%)
  local copies, waits for them, and re-layouts  1.73 us (6%)
    pallas_call x1, Pallas kernels, per_device(): pl.pallas_call(functools.partial(kernel, cx, cy), out_shape=vmem(3, nx +...  28.6 us
    broadcast_in_dim x1, local copies, waits for them, and re-layouts, per_device(): return padded[None, :, XB:XB + nx, YB:YB + ny, :]  1.73 us

profile of v4, /device:TPU:20, one launch (start us, length us, event | category | flops | bytes accessed | tf_op | source)
XLA Modules:
  0.0 30.4 jit_solution(10341591180047990075)
XLA Ops:
  0.0 28.6 %nest_step.1 = f32[3,40,64,90]{3,2,1,0:T(8,128)S(1)} custom-call(f32[1,3,36,48,90]{4,3,2,1,0:T(8,128)} %state.1, f32[1,36,48,90]{3,2,1,0:T(8,128)} %courant.1, f32[90,1,90]{2,1,0:T(1,128)} %bitcast.11, s32[36,4,48]{2,1,0:T(4,128)} %bitcast.7, f32[36,4,48]{2,1,0:T(4,128)} %bitcast.8, s32[9,12,16]{2,1,0:T(8,128)} %bitcast.9, f32[9,12,16]{2,1,0:T(8,128)} %bitcast.10), custom_call_target="tpu_custom_call" | custom-call | tf_op jit(solution)/shard_map/nest_step/pallas_call | solution.py:784
  28.6 1.7 %slice_bitcast_fusion = f32[1,3,36,48,90]{4,3,2,1,0:T(8,128)} fusion(f32[3,40,64,90]{3,2,1,0:T(8,128)S(1)} %nest_step.1), kind=kLoop, calls=%fused_computation | loop fusion | bytes 3732480 | tf_op jit(solution)/shard_map/broadcast_in_dim | solution.py:838

commit v5 on v4

--- a/solution.py
+++ b/solution.py
@@ -315,9 +315,8 @@
         n = 3 * i + j
         return hop(src, fb.at[n, c, part], device, send, fb_recv.at[n, min(c, 1)])
 
-    def pressure_home():
-        whole = slice(0, 3 * quarter)
-        return home(rst.at[0], 0, whole, a % 3, b % 3, (0, to_a, to_b), fb_send.at[0])
+    def pressure_home(part):
+        return home(rst.at[0, part], 0, part, a % 3, b % 3, (0, to_a, to_b), fb_send.at[0])
 
     def fb_start(n):
         c, part = chunks[n]
@@ -632,6 +631,21 @@
             def _():
                 strip_pack((2,))
                 strip_start(slice(2, 3))
+        outer_tile = (b == 0) | (b == cy - 1)
+
+        def columns():
+            with jax.named_scope(f"edge_columns{k}"):
+                edge_columns()
+
+        if last:
+            columns()
+
+            @pl.when(g == 1)
+            def _():
+                restrict(0, range(1, quarter))
+                pressure_home(slice(3, 3 * quarter)).start()
+        else:
+            pl.when(outer_tile)(columns)
         with jax.named_scope(f"receive_x{k}"):
             receive(k, (0, 1))
         edge_winds_x()
@@ -649,10 +663,9 @@
             edge_rows()
             if not last:
                 send_edges(k + 1, (0, 1))
-        with jax.named_scope(f"edge_columns{k}"):
-            edge_columns()
-            if not last:
-                send_edges(k + 1, (2, 3))
+        if not last:
+            pl.when(jnp.logical_not(outer_tile))(columns)
+            send_edges(k + 1, (2, 3))
 
     def take(i, j, comps):
         first, count = comps[0], len(comps)
@@ -676,8 +689,8 @@
     @pl.when(g == 1)
     def _():
         with jax.named_scope("restrict_pressure"):
-            restrict(0, range(quarter))
-        pressure_home().start()
+            restrict(0, (0,))
+        pressure_home(slice(0, 3)).start()
         halo_sent(SUBS - 1)
         x_low, x_high = a == 0, a == cx - 1
         y_low, y_high = b == 0, b == cy - 1
@@ -768,6 +781,15 @@
                 take(i, j, comps)
 
         strips_sent()
+
+
+def store(padded, out, sem):
+    nx, ny = out.shape[2], out.shape[3]
+    copy = pltpu.make_async_copy(
+        padded.at[:, pl.ds(XB, nx), pl.ds(YB, ny), :], out.at[0], sem.at[0]
+    )
+    copy.start()
+    copy.wait()
 
 
 def per_device(
@@ -835,7 +857,11 @@
         interp_index.transpose(0, 2, 1), interp_weight.transpose(0, 2, 1),
         restrict_index.transpose(2, 0, 1), restrict_weight.transpose(2, 0, 1),
     )
-    return padded[None, :, XB : XB + nx, YB : YB + ny, :]
+    return pl.pallas_call(
+        store, out_shape=jax.ShapeDtypeStruct(state.shape, F32), in_specs=[inside], out_specs=anywhere,
+        scratch_shapes=[dma((1,))], name="store",
+        compiler_params=pltpu.CompilerParams(vmem_limit_bytes=2**20),
+    )(padded)
 
 
 def solution(mesh):

time: 30.5 us -> 30 us (0.984)
  local copies, waits for them, and re-layouts: 1.73 us -> 0 us
  Pallas kernels: 28.6 us -> 29.9 us
    broadcast_in_dim x1 -> x0, local copies, waits for them, and re-layouts: 1.73 us -> none  [per_device(): return padded[None, :, XB:XB + nx, YB:YB + ny, :]]
    pallas_call x0 -> x1, Pallas kernels: none -> 1.51 us  [per_device(): pl.pallas_call(store, out_shape=jax.ShapeDtypeStruct(state.shape, F32), i...]
where the time goes in v5:
time: 30 us; the launch traced here: 29.9 us
  Pallas kernels  29.9 us (100%)
    pallas_call x1, Pallas kernels, per_device(): pl.pallas_call(functools.partial(kernel, cx, cy), out_shape=vmem(3, nx +...  28.4 us
    pallas_call x1, Pallas kernels, per_device(): pl.pallas_call(store, out_shape=jax.ShapeDtypeStruct(state.shape, F32), i...  1.51 us

profile of v5, /device:TPU:20, one launch (start us, length us, event | category | flops | bytes accessed | tf_op | source)
XLA Modules:
  0.0 29.9 jit_solution(8984404611043596327)
XLA Ops:
  0.0 28.4 %nest_step.1.padded = f32[3,40,64,90]{3,2,1,0:T(8,128)S(1)} custom-call(f32[1,3,36,48,90]{4,3,2,1,0:T(8,128)} %state.1, f32[1,36,48,90]{3,2,1,0:T(8,128)} %courant.1, f32[90,1,90]{2,1,0:T(1,128)} %bitcast.9, s32[36,4,48]{2,1,0:T(4,128)} %bitcast.5, f32[36,4,48]{2,1,0:T(4,128)} %bitcast.6, s32[9,12,16]{2,1,0:T(8,128)} %bitcast.7, f32[9,12,16]{2,1,0:T(8,128)} %bitcast.8), custom_call_target="tpu_custom_call" | custom-call | tf_op jit(solution)/shard_map/nest_step/pallas_call | solution.py:806
  28.4 1.5 %store.1 = f32[1,3,36,48,90]{4,3,2,1,0:T(8,128)} custom-call(f32[3,40,64,90]{3,2,1,0:T(8,128)S(1)} %nest_step.1.padded), custom_call_target="tpu_custom_call" | custom-call | tf_op jit(solution)/shard_map/store/pallas_call | solution.py:860

commit v6 on v5

--- a/solution.py
+++ b/solution.py
@@ -313,10 +313,13 @@
 
     def home(src, c, part, i, j, device, send):
         n = 3 * i + j
-        return hop(src, fb.at[n, c, part], device, send, fb_recv.at[n, min(c, 1)])
+        return hop(src, fb.at[n, c, part], device, send, fb_recv.at[i, min(c, 1)])
 
     def pressure_home(part):
         return home(rst.at[0, part], 0, part, a % 3, b % 3, (0, to_a, to_b), fb_send.at[0])
+
+    def q_slot(at, n):
+        return 6 * n + at
 
     def fb_start(n):
         c, part = chunks[n]
@@ -330,7 +333,7 @@
         @pl.when(around)
         def _():
             at = jnp.where(back, 0, 3) + b % 3
-            hop(mine, q0.at[at, c - 1, part], (0, relay_a, to_b), sem, q_recv.at[at, n]).start()
+            hop(mine, q0.at[at, c - 1, part], (0, relay_a, to_b), sem, q_recv.at[q_slot(at, n)]).start()
 
     def pass_on():
         for n, (c, part) in enumerate(chunks):
@@ -338,7 +341,7 @@
                 @pl.when(on)
                 def _():
                     piece = q0.at[at, c - 1, part]
-                    hop(piece, piece, (g, a, b), q_send.at[at], q_recv.at[at, n]).wait_recv()
+                    hop(piece, piece, (g, a, b), q_send.at[at], q_recv.at[q_slot(at, n)]).wait_recv()
                     home(piece, c, part, i, j, (0, home_a, b), q_send.at[at]).start()
 
     def passed_on():
@@ -347,7 +350,7 @@
             def _():
                 sent = [q0.at[at]] if at < 3 else [q0.at[at, 0, chunks[0][1]], q0.at[at, 1]]
                 for piece in sent:
-                    hop(piece, piece, (g, a, b), q_send.at[at], q_recv.at[0, 0]).wait_send()
+                    hop(piece, piece, (g, a, b), q_send.at[at], q_recv.at[0]).wait_send()
 
     def rows_of(i):
         if i == 0:
@@ -483,7 +486,7 @@
                 child = 3 * (b - fy) + j
                 yield here & (child < cy), pltpu.make_async_remote_copy(
                     src_ref=xpack.at[comps, :, pl.ds(j * ty, ty), :], dst_ref=xstrip.at[comps],
-                    send_sem=strip_send.at[0, j], recv_sem=strip_recv.at[0, 0],
+                    send_sem=strip_send.at[j], recv_sem=strip_recv.at[0, 0],
                     device_id=(1, edge, child), device_id_type=MESH,
                 )
                 if comps.start > 0:
@@ -501,7 +504,7 @@
                 yield here & (child >= 0) & (child < cx), pltpu.make_async_remote_copy(
                     src_ref=ypack.at[comps, pl.ds(lo, hi - lo)],
                     dst_ref=ystrip.at[comps, pl.ds(dst, hi - lo)],
-                    send_sem=strip_send.at[1, i + 1], recv_sem=strip_recv.at[1, kinds[i]],
+                    send_sem=strip_send.at[4 + i], recv_sem=strip_recv.at[1, kinds[i]],
                     device_id=(1, child, edge), device_id_type=MESH,
                 )
 
@@ -519,7 +522,7 @@
 
     def strip_wait(ref, kind):
         pltpu.make_async_remote_copy(
-            src_ref=ref, dst_ref=ref, send_sem=strip_send.at[0, 0],
+            src_ref=ref, dst_ref=ref, send_sem=strip_send.at[0],
             recv_sem=strip_recv.at[kind], device_id=(g, a, b), device_id_type=MESH,
         ).wait_recv()
 
@@ -667,15 +670,17 @@
             pl.when(jnp.logical_not(outer_tile))(columns)
             send_edges(k + 1, (2, 3))
 
+    def arrived(i, comps):
+        first = comps[0]
+        for count in range(1, 4):
+            here = (a >= fx) & (b >= fy) & (3 * (a - fx) + i < cx)
+
+            @pl.when(here & (jnp.minimum(cy - 3 * (b - fy), 3) == count))
+            def _():
+                row = fb.at[3 * i : 3 * i + count, first : first + len(comps)]
+                hop(row, row, (g, a, b), fb_send.at[0], fb_recv.at[i, min(first, 1)]).wait_recv()
+
     def take(i, j, comps):
-        first, count = comps[0], len(comps)
-        with jax.named_scope(f"piece{i}{j}{first}"):
-            piece = fb.at[3 * i + j, first : first + count]
-            pltpu.make_async_remote_copy(
-                src_ref=piece, dst_ref=piece, send_sem=fb_send.at[0],
-                recv_sem=fb_recv.at[3 * i + j, min(first, 1)], device_id=(g, a, b),
-                device_id_type=MESH,
-            ).wait_recv()
         for c in comps:
             for n in range(quarter):
                 got = fb[3 * i + j, c, 3 * n : 3 * n + 3]
@@ -757,7 +762,7 @@
 
         for part, comps in ((1, slice(1, 3)), (0, slice(0, 1))):
             piece = rst.at[comps]
-            hop(piece, piece, (g, a, b), fb_send.at[part], q_recv.at[0, 0]).wait_send()
+            hop(piece, piece, (g, a, b), fb_send.at[part], q_recv.at[0]).wait_send()
 
     @pl.when(g == 0)
     def _():
@@ -768,17 +773,17 @@
         halo_sent(SUBS - 1)
         passed_on()
         winds_of, pressure_of = (1, 2), (0,)
-        tiles = [[(i, j) for j in (2, 0, 1)] for i in range(3)]
-        order = [(at, winds_of) for at in tiles[1]] + [(at, pressure_of) for at in tiles[1]]
-        order += [(at, winds_of) for at in tiles[2]] + [(at, pressure_of) for at in tiles[0]]
-        order += [(at, pressure_of) for at in tiles[2][:2]] + [(at, winds_of) for at in tiles[0]]
-        order += [(at, pressure_of) for at in tiles[2][2:]]
-        for (i, j), comps in order:
-            there = (a >= fx) & (b >= fy) & (3 * (a - fx) + i < cx) & (3 * (b - fy) + j < cy)
-
-            @pl.when(there)
-            def _():
-                take(i, j, comps)
+        for i, comps in (
+            (1, winds_of), (1, pressure_of), (2, winds_of), (0, pressure_of), (2, pressure_of), (0, winds_of)
+        ):
+            with jax.named_scope(f"row{i}{comps[0]}"):
+                arrived(i, comps)
+            for j in range(3):
+                there = (a >= fx) & (b >= fy) & (3 * (a - fx) + i < cx) & (3 * (b - fy) + j < cy)
+
+                @pl.when(there)
+                def _():
+                    take(i, j, comps)
 
         strips_sent()
 
@@ -836,16 +841,16 @@
             dma((7,)),
             dma((4,)),
             dma((2, 4)),
-            dma((2, 5)),
+            dma((8,)),
             dma((2, 3)),
             dma((2,)),
-            dma((9, 2)),
+            dma((3, 2)),
             vmem(6, 2, *packed),
             vmem(3, 3, ny, lev),
             vmem(2, 3, 3, 4, lev),
             vmem(3, nx, 4, lev),
             dma((6,)),
-            dma((6, 3)),
+            dma((15,)),
             dma((2, 3)),
         ],
         compiler_params=pltpu.CompilerParams(

time: 30 us -> 29.8 us (level)
  no operation moved by 1% of the time
where the time goes in v6:
time: 29.8 us; the launch traced here: 29.7 us
  Pallas kernels  29.7 us (100%)
    pallas_call x1, Pallas kernels, per_device(): pl.pallas_call(functools.partial(kernel, cx, cy), out_shape=vmem(3, nx +...  28.2 us
    pallas_call x1, Pallas kernels, per_device(): pl.pallas_call(store, out_shape=jax.ShapeDtypeStruct(state.shape, F32), i...  1.51 us

profile of v6, /device:TPU:20, one launch (start us, length us, event | category | flops | bytes accessed | tf_op | source)
XLA Modules:
  0.0 29.7 jit_solution(1691591762034795995)
XLA Ops:
  0.0 28.2 %nest_step.1.padded = f32[3,40,64,90]{3,2,1,0:T(8,128)S(1)} custom-call(f32[1,3,36,48,90]{4,3,2,1,0:T(8,128)} %state.1, f32[1,36,48,90]{3,2,1,0:T(8,128)} %courant.1, f32[90,1,90]{2,1,0:T(1,128)} %bitcast.9, s32[36,4,48]{2,1,0:T(4,128)} %bitcast.5, f32[36,4,48]{2,1,0:T(4,128)} %bitcast.6, s32[9,12,16]{2,1,0:T(8,128)} %bitcast.7, f32[9,12,16]{2,1,0:T(8,128)} %bitcast.8), custom_call_target="tpu_custom_call" | custom-call | tf_op jit(solution)/shard_map/nest_step/pallas_call | solution.py:811
  28.2 1.5 %store.1 = f32[1,3,36,48,90]{4,3,2,1,0:T(8,128)} custom-call(f32[3,40,64,90]{3,2,1,0:T(8,128)S(1)} %nest_step.1.padded), custom_call_target="tpu_custom_call" | custom-call | tf_op jit(solution)/shard_map/store/pallas_call | solution.py:865

commit v7 on v6

--- a/solution.py
+++ b/solution.py
@@ -615,11 +615,6 @@
 
         with jax.named_scope(f"inner_pressure{k}"):
             inner_pressure()
-        if k == 1:
-            @pl.when((g == 1) & ((a == 0) | (a == cx - 1) | (b == 0) | (b == cy - 1)))
-            def _():
-                with jax.named_scope("boundary_weights"):
-                    boundary_weights()
         with jax.named_scope(f"receive_y{k}"):
             receive(k, (2, 3))
         edge_winds_y()
@@ -696,6 +691,12 @@
         with jax.named_scope("restrict_pressure"):
             restrict(0, (0,))
         pressure_home(slice(0, 3)).start()
+
+        @pl.when((a == 0) | (a == cx - 1) | (b == 0) | (b == cy - 1))
+        def _():
+            with jax.named_scope("boundary_weights"):
+                boundary_weights()
+
         halo_sent(SUBS - 1)
         x_low, x_high = a == 0, a == cx - 1
         y_low, y_high = b == 0, b == cy - 1

time: 29.8 us -> 29.8 us (level)
  no operation moved by 1% of the time
where the time goes in v7:
time: 29.8 us; the launch traced here: 29.7 us
  Pallas kernels  29.7 us (100%)
    pallas_call x1, Pallas kernels, per_device(): pl.pallas_call(functools.partial(kernel, cx, cy), out_shape=vmem(3, nx +...  28.2 us
    pallas_call x1, Pallas kernels, per_device(): pl.pallas_call(store, out_shape=jax.ShapeDtypeStruct(state.shape, F32), i...  1.51 us

profile of v7, /device:TPU:20, one launch (start us, length us, event | category | flops | bytes accessed | tf_op | source)
XLA Modules:
  0.0 29.7 jit_solution(3231896521288052138)
XLA Ops:
  0.0 28.2 %nest_step.1.padded = f32[3,40,64,90]{3,2,1,0:T(8,128)S(1)} custom-call(f32[1,3,36,48,90]{4,3,2,1,0:T(8,128)} %state.1, f32[1,36,48,90]{3,2,1,0:T(8,128)} %courant.1, f32[90,1,90]{2,1,0:T(1,128)} %bitcast.9, s32[36,4,48]{2,1,0:T(4,128)} %bitcast.5, f32[36,4,48]{2,1,0:T(4,128)} %bitcast.6, s32[9,12,16]{2,1,0:T(8,128)} %bitcast.7, f32[9,12,16]{2,1,0:T(8,128)} %bitcast.8), custom_call_target="tpu_custom_call" | custom-call | tf_op jit(solution)/shard_map/nest_step/pallas_call | solution.py:812
  28.2 1.5 %store.1 = f32[1,3,36,48,90]{4,3,2,1,0:T(8,128)} custom-call(f32[3,40,64,90]{3,2,1,0:T(8,128)S(1)} %nest_step.1.padded), custom_call_target="tpu_custom_call" | custom-call | tf_op jit(solution)/shard_map/store/pallas_call | solution.py:866
